TPU v7x, 32 devices: a whole 2x2x4 slice. The times are simulated.
32 devices in a mesh: tok: 8 (over z, y), vocab: 4 (over x, core).
Axes of the slice: x: 2, y: 2, z: 4, core: 2. Of those that a mesh axis runs over, the one named last changes fastest.
Arguments:
- hidden: bfloat16 [192, 9216], P('tok'), may hold values from -256 to 256
- policy_head: bfloat16 [9216, 32768], P(None, ('tok', 'vocab')), may hold values from -0.0625 to 0.0625
- reference_head: bfloat16 [9216, 32768], P(None, ('tok', 'vocab')), may hold values from -0.0625 to 0.0625
- targets: int32 [192], P('tok'), may hold values from 0 to 32767
Outputs:
- policy_logprob: float32 [192], P('tok')
- reference_logprob: float32 [192], P('tok')
- divergence: float32 [192], P('tok')
All inputs are finite; a program needn't handle non-finite values.
Results may differ from a plain program's by a relative error of at most 0.00055.
Values may be sent and summed in bfloat16 or wider, within the bound.
No kernel may reach another device: no remote copies, remote signals or barrier semaphores. Data moves between devices by JAX's collectives and lax.ppermute only.
A program may use at most 128 MiB of HBM per device.

v0:
```python
import jax
import jax.numpy as jnp
from jax import lax
from jax.sharding import PartitionSpec as P


def combined_all(value, axis, combine):
    everything = jax.tree.map(lambda part: lax.all_gather(part, axis), value)
    leading = jax.tree.map(lambda part: part[0], everything)

    def step(k, so_far):
        return combine(so_far, jax.tree.map(lambda part: part[k], everything))

    return lax.fori_loop(1, lax.axis_size(axis), step, leading)


def local_sums(policy_logits, reference_logits, target_hits, peak_policy, peak_reference):
    policy_exp = jnp.exp(policy_logits - peak_policy[:, None])
    reference_exp = jnp.exp(reference_logits - peak_reference[:, None])
    total_policy = jnp.sum(policy_exp, axis=1)
    total_reference = jnp.sum(reference_exp, axis=1)
    weighted = jnp.sum(policy_exp * (policy_logits - reference_logits), axis=1)
    target_policy = jnp.sum(jnp.where(target_hits, policy_logits, 0.0), axis=1)
    target_reference = jnp.sum(jnp.where(target_hits, reference_logits, 0.0), axis=1)
    return (total_policy, total_reference, weighted, target_policy, target_reference)


def local_stats(policy_logits, reference_logits, target_hits):
    peak_policy = jnp.max(policy_logits, axis=1)
    peak_reference = jnp.max(reference_logits, axis=1)
    summed = local_sums(policy_logits, reference_logits, target_hits, peak_policy, peak_reference)
    return (peak_policy, peak_reference) + summed


def combine_stats(left_stats, right_stats):
    peak_policy = jnp.maximum(left_stats[0], right_stats[0])
    peak_reference = jnp.maximum(left_stats[1], right_stats[1])
    left_policy = jnp.exp(left_stats[0] - peak_policy)
    right_policy = jnp.exp(right_stats[0] - peak_policy)
    left_reference = jnp.exp(left_stats[1] - peak_reference)
    right_reference = jnp.exp(right_stats[1] - peak_reference)
    return (
        peak_policy,
        peak_reference,
        left_stats[2] * left_policy + right_stats[2] * right_policy,
        left_stats[3] * left_reference + right_stats[3] * right_reference,
        left_stats[4] * left_policy + right_stats[4] * right_policy,
        left_stats[5] + right_stats[5],
        left_stats[6] + right_stats[6],
    )


def combine_senders(received):
    peak_policy = jnp.max(received[0], axis=0)
    peak_reference = jnp.max(received[1], axis=0)
    policy_scale = jnp.exp(received[0] - peak_policy[None, :])
    reference_scale = jnp.exp(received[1] - peak_reference[None, :])
    return (
        peak_policy,
        peak_reference,
        jnp.sum(received[2] * policy_scale, axis=0),
        jnp.sum(received[3] * reference_scale, axis=0),
        jnp.sum(received[4] * policy_scale, axis=0),
        jnp.sum(received[5], axis=0),
        jnp.sum(received[6], axis=0),
    )


def finish(merged_stats):
    log_norm_policy = merged_stats[0] + jnp.log(merged_stats[2])
    log_norm_reference = merged_stats[1] + jnp.log(merged_stats[3])
    policy_logprob = merged_stats[5] - log_norm_policy
    reference_logprob = merged_stats[6] - log_norm_reference
    divergence = merged_stats[4] / merged_stats[2] - log_norm_policy + log_norm_reference
    return (policy_logprob, reference_logprob, divergence)


def body(hidden, policy_head, reference_head, targets):
    tok_count = lax.axis_size("tok")
    vocab_count = lax.axis_size("vocab")
    tok_rows = hidden.shape[0]
    vocab_cols = policy_head.shape[1]
    piece = lax.all_gather(hidden, "tok", axis=0, tiled=True)
    summed = jnp.concatenate(
        [
            jnp.dot(piece, policy_head, preferred_element_type=jnp.float32),
            jnp.dot(piece, reference_head, preferred_element_type=jnp.float32),
        ],
        axis=1,
    )
    policy_logits = summed[:, :vocab_cols]
    reference_logits = summed[:, vocab_cols:]
    every_target = lax.all_gather(targets, "tok", axis=0, tiled=True)
    block_index = lax.axis_index("tok") * vocab_count + lax.axis_index("vocab")
    vocab_ids = block_index * vocab_cols + lax.iota(jnp.int32, vocab_cols)
    target_hits = vocab_ids[None, :] == every_target[:, None]
    partial_value = local_stats(policy_logits, reference_logits, target_hits)
    shaped = tuple((entry.reshape(tok_count, tok_rows) for entry in partial_value))
    received = lax.all_to_all(shaped, "tok", split_axis=0, concat_axis=0, tiled=True)
    own_stats = combine_senders(received)
    merged_stats = combined_all(own_stats, "vocab", combine_stats)
    return finish(merged_stats)


def solution(mesh):
    in_specs = (P("tok", None), P(None, ("tok", "vocab")), P(None, ("tok", "vocab")), P("tok"))
    out_specs = (P("tok"), P("tok"), P("tok"))
    return jax.shard_map(body, mesh=mesh, in_specs=in_specs, out_specs=out_specs, check_vma=False)
```

profile of v0, /device:TPU:0, one launch (start us, length us, event | category | flops | bytes accessed | tf_op | source)
XLA Modules:
  0.0 179.8 jit_solution(15287167651976823062)
XLA Ops:
  7.2 0.7 all-gather.9.cloned.1.call-update
  7.9 1.2 dynamic-slice.5
  9.8 0.9 dynamic-update-slice.5
  10.7 13.1 %all-reduce.5 = s32[192]{0:T(256)S(1)} all-reduce(s32[192]{0:T(256)S(1)} %dynamic-update-slice.5), channel_id=1, replica_groups=mesh['tok'=8,'vocab'=4] {'tok'}, use_global_device_ids=true, to_apply=%add.5 | all-reduce | flops 192 | bytes 1536
  23.8 53.8 %all-gather.9.cloned.1.call-done = bf16[192,9216]{1,0:T(8,128)(2,1)} async-done(((bf16[24,9216]{1,0:T(8,128)(2,1)}), bf16[192,9216]{1,0:T(8,128)(2,1)}) %all-gather.9.cloned.1.call-update) | async-done | bytes 3538960 | tf_op jit(solution)/shard_map/all_gather | solution.py:83
  77.5 9.6 %fusion.24 = (f32[192]{0:T(256)S(1)}, f32[192,1024]{1,0:T(8,128)S(1)}) fusion(bf16[192,9216]{1,0:T(8,128)(2,1)} %all-gather.9.cloned.1.call-done, bf16[9216,1024]{1,0:T(8,128)(2,1)} %param.7), kind=kOutput, calls=%fused_computation.44 | convolution fusion | flops 3624075008 | bytes 23200512 | tf_op jit(solution)/shard_map/dot_general | solution.py:86
  87.2 3.1 %copy-done = bf16[9216,1024]{1,0:T(8,128)(2,1)S(1)} copy-done((bf16[9216,1024]{1,0:T(8,128)(2,1)S(1)}, bf16[9216,1024]{1,0:T(8,128)(2,1)}, u32[]{:S(2)}) %copy-start) | copy-done | bytes 18874392
  90.3 5.9 %fusion.25 = (f32[192]{0:T(256)S(1)}, f32[192,1024]{1,0:T(8,128)S(1)}) fusion(bf16[192,9216]{1,0:T(8,128)(2,1)} %all-gather.9.cloned.1.call-done, bf16[9216,1024]{1,0:T(8,128)(2,1)S(1)} %copy-done), kind=kOutput, calls=%fused_computation.45 | convolution fusion | flops 3624075008 | bytes 23200512 | tf_op jit(solution)/shard_map/dot_general | solution.py:87
  96.2 0.7 multiply_reduce_fusion
  96.9 0.7 all_to_all.64
  97.5 3.3 %all-to-all-start.4 = ((f32[8,1,24]{2,1,0:T(1,128)}), f32[8,1,24]{2,1,0:T(1,128)S(1)}, u32[]{:S(2)}, u32[]{:S(2)}) async-start(f32[8,1,24]{2,1,0:T(1,128)} %all_to_all.64), calls=%async_computation.4 | async-start | bytes 8192 | tf_op jit(solution)/shard_map/all_to_all | solution.py:99
  100.9 0.7 all_to_all.56
  101.6 5.8 %all-to-all-done.4 = f32[8,1,24]{2,1,0:T(1,128)S(1)} async-done(((f32[8,1,24]{2,1,0:T(1,128)}), f32[8,1,24]{2,1,0:T(1,128)S(1)}, u32[]{:S(2)}, u32[]{:S(2)}) %all-to-all-start.4) | async-done | bytes 800 | tf_op jit(solution)/shard_map/all_to_all | solution.py:99
  107.4 3.2 %all-to-all-start.2 = ((f32[8,1,24]{2,1,0:T(1,128)}), f32[8,1,24]{2,1,0:T(1,128)S(1)}, u32[]{:S(2)}, u32[]{:S(2)}) async-start(f32[8,1,24]{2,1,0:T(1,128)} %all_to_all.56), calls=%async_computation.2 | async-start | bytes 8192 | tf_op jit(solution)/shard_map/all_to_all | solution.py:99
  110.6 0.7 all_to_all.52
  111.3 5.7 %all-to-all-done.2 = f32[8,1,24]{2,1,0:T(1,128)S(1)} async-done(((f32[8,1,24]{2,1,0:T(1,128)}), f32[8,1,24]{2,1,0:T(1,128)S(1)}, u32[]{:S(2)}, u32[]{:S(2)}) %all-to-all-start.2) | async-done | bytes 800 | tf_op jit(solution)/shard_map/all_to_all | solution.py:99
  117.1 3.3 %all-to-all-start = ((f32[8,1,24]{2,1,0:T(1,128)}), f32[8,1,24]{2,1,0:T(1,128)S(1)}, u32[]{:S(2)}, u32[]{:S(2)}) async-start(f32[8,1,24]{2,1,0:T(1,128)} %all_to_all.52), calls=%async_computation | async-start | bytes 8192 | tf_op jit(solution)/shard_map/all_to_all | solution.py:99
  120.4 0.7 all_to_all.60
  121.1 5.8 %all-to-all-done = f32[8,1,24]{2,1,0:T(1,128)S(1)} async-done(((f32[8,1,24]{2,1,0:T(1,128)}), f32[8,1,24]{2,1,0:T(1,128)S(1)}, u32[]{:S(2)}, u32[]{:S(2)}) %all-to-all-start) | async-done | bytes 800 | tf_op jit(solution)/shard_map/all_to_all | solution.py:99
  126.8 3.2 %all-to-all-start.3 = ((f32[8,1,24]{2,1,0:T(1,128)}), f32[8,1,24]{2,1,0:T(1,128)S(1)}, u32[]{:S(2)}, u32[]{:S(2)}) async-start(f32[8,1,24]{2,1,0:T(1,128)} %all_to_all.60), calls=%async_computation.3 | async-start | bytes 8192 | tf_op jit(solution)/shard_map/all_to_all | solution.py:99
  130.1 0.7 all_to_all.54
  130.8 5.7 %all-to-all-done.3 = f32[8,1,24]{2,1,0:T(1,128)S(1)} async-done(((f32[8,1,24]{2,1,0:T(1,128)}), f32[8,1,24]{2,1,0:T(1,128)S(1)}, u32[]{:S(2)}, u32[]{:S(2)}) %all-to-all-start.3) | async-done | bytes 800 | tf_op jit(solution)/shard_map/all_to_all | solution.py:99
  136.5 3.3 %all-to-all-start.1 = ((f32[8,1,24]{2,1,0:T(1,128)}), f32[8,1,24]{2,1,0:T(1,128)S(1)}, u32[]{:S(2)}, u32[]{:S(2)}) async-start(f32[8,1,24]{2,1,0:T(1,128)} %all_to_all.54), calls=%async_computation.1 | async-start | bytes 8192 | tf_op jit(solution)/shard_map/all_to_all | solution.py:99
  139.9 0.6 dynamic-slice
  141.1 0.7 all_to_all.67
  141.8 0.7 all_to_all.69
  142.5 3.8 %all-to-all-done.1 = f32[8,1,24]{2,1,0:T(1,128)S(1)} async-done(((f32[8,1,24]{2,1,0:T(1,128)}), f32[8,1,24]{2,1,0:T(1,128)S(1)}, u32[]{:S(2)}, u32[]{:S(2)}) %all-to-all-start.1) | async-done | bytes 800 | tf_op jit(solution)/shard_map/all_to_all | solution.py:99
  146.3 3.2 %all-to-all-start.5 = ((f32[8,1,24]{2,1,0:T(1,128)}), f32[8,1,24]{2,1,0:T(1,128)S(1)}, u32[]{:S(2)}, u32[]{:S(2)}) async-start(f32[8,1,24]{2,1,0:T(1,128)} %all_to_all.67), calls=%async_computation.5 | async-start | bytes 8192 | tf_op jit(solution)/shard_map/all_to_all | solution.py:99
  149.6 6.4 %all-to-all-done.5 = f32[8,1,24]{2,1,0:T(1,128)S(1)} async-done(((f32[8,1,24]{2,1,0:T(1,128)}), f32[8,1,24]{2,1,0:T(1,128)S(1)}, u32[]{:S(2)}, u32[]{:S(2)}) %all-to-all-start.5) | async-done | bytes 800 | tf_op jit(solution)/shard_map/all_to_all | solution.py:99
  156.0 3.3 %all-to-all-start.6 = ((f32[8,1,24]{2,1,0:T(1,128)}), f32[8,1,24]{2,1,0:T(1,128)S(1)}, u32[]{:S(2)}, u32[]{:S(2)}) async-start(f32[8,1,24]{2,1,0:T(1,128)} %all_to_all.69), calls=%async_computation.6 | async-start | bytes 8192 | tf_op jit(solution)/shard_map/all_to_all | solution.py:99
  159.3 0.2 dynamic-update-slice
  159.5 0.2 dynamic-update-slice.1
  159.7 0.2 dynamic-update-slice.4
  159.9 0.2 dynamic-update-slice.2
  160.1 0.2 dynamic-update-slice.3
  160.4 0.2 dynamic-update-slice.6
  160.6 5.1 %all-to-all-done.6 = f32[8,1,24]{2,1,0:T(1,128)S(1)} async-done(((f32[8,1,24]{2,1,0:T(1,128)}), f32[8,1,24]{2,1,0:T(1,128)S(1)}, u32[]{:S(2)}, u32[]{:S(2)}) %all-to-all-start.6) | async-done | bytes 800 | tf_op jit(solution)/shard_map/all_to_all | solution.py:99
  165.7 0.2 dynamic-update-slice.7
  165.9 5.6 %all-reduce.8 = (f32[96]{0:T(128)S(1)}, f32[96]{0:T(128)S(1)}, f32[96]{0:T(128)S(1)}, f32[96]{0:T(128)S(1)}, f32[96]{0:T(128)S(1)}, /*index=5*/f32[96]{0:T(128)S(1)}, f32[96]{0:T(128)S(1)}) all-reduce(f32[96]{0:T(128)S(1)} %dynamic-update-slice, f32[96]{0:T(128)S(1)} %dynamic-update-slice.1, ...), channel_id=2, replica_groups=mesh['tok'=8,'vocab'=4] {'vocab'}, use_global_device_ids=true, to_apply=%add | all-reduce | flops 672 | bytes 5376
  171.6 0.1 reshape.43
  171.7 0.1 reshape.44
  171.7 0.1 reshape.45
  171.8 0.1 reshape.46
  171.9 0.1 reshape.47
  172.0 0.1 reshape.48
  172.1 0.1 reshape.49
  172.2 0.3 while.27
  172.5 0.5 subtract_add_fusion
  (31 shorter events, 0.4 us)
Async XLA Ops:
  7.2 70.3 %all-gather.9.cloned.1.call-start = ((), (), s32[]{:S(2)}) async-start(), calls=%async_computation.7 | async-start | bytes 3981312 | tf_op jit(solution)/shard_map/all_gather | solution.py:83
  77.5 12.7 %copy-start = (bf16[9216,1024]{1,0:T(8,128)(2,1)S(1)}, bf16[9216,1024]{1,0:T(8,128)(2,1)}, u32[]{:S(2)}) copy-start(bf16[9216,1024]{1,0:T(8,128)(2,1)} %param.8) | copy-start | bytes 56623108
  90.3 49.6 %copy-start.1 = (u32[32]{0:T(128)S(1)}, u32[32]{0:T(128)}, u32[]{:S(2)}) copy-start(u32[32]{0:T(128)} %constant.57) | copy-start | bytes 388
  97.5 9.8 %all-to-all-start.4 = ((f32[8,1,24]{2,1,0:T(1,128)}), f32[8,1,24]{2,1,0:T(1,128)S(1)}, u32[]{:S(2)}, u32[]{:S(2)}) async-start(f32[8,1,24]{2,1,0:T(1,128)} %all_to_all.64), calls=%async_computation.4 | async-start | bytes 8192 | tf_op jit(solution)/shard_map/all_to_all | solution.py:99
  107.4 9.7 %all-to-all-start.2 = ((f32[8,1,24]{2,1,0:T(1,128)}), f32[8,1,24]{2,1,0:T(1,128)S(1)}, u32[]{:S(2)}, u32[]{:S(2)}) async-start(f32[8,1,24]{2,1,0:T(1,128)} %all_to_all.56), calls=%async_computation.2 | async-start | bytes 8192 | tf_op jit(solution)/shard_map/all_to_all | solution.py:99
  117.1 9.8 %all-to-all-start = ((f32[8,1,24]{2,1,0:T(1,128)}), f32[8,1,24]{2,1,0:T(1,128)S(1)}, u32[]{:S(2)}, u32[]{:S(2)}) async-start(f32[8,1,24]{2,1,0:T(1,128)} %all_to_all.52), calls=%async_computation | async-start | bytes 8192 | tf_op jit(solution)/shard_map/all_to_all | solution.py:99
  126.8 9.7 %all-to-all-start.3 = ((f32[8,1,24]{2,1,0:T(1,128)}), f32[8,1,24]{2,1,0:T(1,128)S(1)}, u32[]{:S(2)}, u32[]{:S(2)}) async-start(f32[8,1,24]{2,1,0:T(1,128)} %all_to_all.60), calls=%async_computation.3 | async-start | bytes 8192 | tf_op jit(solution)/shard_map/all_to_all | solution.py:99
  136.5 9.8 %all-to-all-start.1 = ((f32[8,1,24]{2,1,0:T(1,128)}), f32[8,1,24]{2,1,0:T(1,128)S(1)}, u32[]{:S(2)}, u32[]{:S(2)}) async-start(f32[8,1,24]{2,1,0:T(1,128)} %all_to_all.54), calls=%async_computation.1 | async-start | bytes 8192 | tf_op jit(solution)/shard_map/all_to_all | solution.py:99
  146.3 9.7 %all-to-all-start.5 = ((f32[8,1,24]{2,1,0:T(1,128)}), f32[8,1,24]{2,1,0:T(1,128)S(1)}, u32[]{:S(2)}, u32[]{:S(2)}) async-start(f32[8,1,24]{2,1,0:T(1,128)} %all_to_all.67), calls=%async_computation.5 | async-start | bytes 8192 | tf_op jit(solution)/shard_map/all_to_all | solution.py:99
  156.0 9.7 %all-to-all-start.6 = ((f32[8,1,24]{2,1,0:T(1,128)}), f32[8,1,24]{2,1,0:T(1,128)S(1)}, u32[]{:S(2)}, u32[]{:S(2)}) async-start(f32[8,1,24]{2,1,0:T(1,128)} %all_to_all.69), calls=%async_computation.6 | async-start | bytes 8192 | tf_op jit(solution)/shard_map/all_to_all | solution.py:99
Sparse Core Ops, SparseCore 0:
  10.2 67.3 all-gather.8
where the time goes:
time: 180 us
  waiting for transfers between devices  92.7 us (52%)
  starting transfers between devices  23.1 us (13%)
  blocking collectives  18.7 us (10%)
  matrix products  15.6 us (9%)
  between operations  15.5 us (9%)
  local copies, waits for them, and re-layouts  12.7 us (7%)
    all_gather x1, waiting for transfers between devices, body(): piece = lax.all_gather(hidden, 'tok', axis=0, tiled=True)  53.8 us
    all_to_all x7, waiting for transfers between devices, body(): lax.all_to_all(shaped, 'tok', split_axis=0, concat_axis=0, tiled=True)  38.3 us
    all_to_all x7, starting transfers between devices, body(): lax.all_to_all(shaped, 'tok', split_axis=0, concat_axis=0, tiled=True)  23 us
    unnamed x2, blocking collectives  18.7 us
    dot_general x1, matrix products, body(): jnp.dot(piece, policy_head, preferred_element_type=jnp.float32)  9.63 us
    unnamed x22, local copies, waits for them, and re-layouts  7.34 us
    dot_general x1, matrix products, body(): jnp.dot(piece, reference_head, preferred_element_type=jnp.float32)  5.92 us
    all_to_all x7, local copies, waits for them, and re-layouts, body(): lax.all_to_all(shaped, 'tok', split_axis=0, concat_axis=0, tiled=True)  4.75 us
  transfers between devices with their start and end apart: 8, of which 8 were waited for; matrix products, arithmetic and copies ran while one was open for 2% of the time, Pallas kernels for 0%

commit v1 on v0

v1 whole, which is shorter than its diff:
```python
import functools

import jax
import jax.numpy as jnp
from jax import lax
from jax.experimental import pallas as pl
from jax.experimental.pallas import tpu as pltpu
from jax.sharding import PartitionSpec as P


LANES = 128
TILE = 512
CHUNK = 768
STATS = 7
SPLIT = 9216
AHEAD = 0
MARGIN = 4 << 20


def hop(value, mask, count):
    pairs = [(i, i ^ mask) for i in range(count)]
    return lax.ppermute(value, ("tok", "vocab"), pairs)


def with_ids(columns, targets):
    digits = jnp.stack([(targets >> (8 * k)) & 255 for k in range(3)], axis=1)
    digits = jnp.pad(digits, ((0, 0), (0, LANES - 3)))
    return jnp.concatenate(columns + [digits.astype(columns[0].dtype)], axis=1)


class Plan:
    def __init__(self, depth, vocab_count):
        unit = vocab_count * LANES
        self.wide = min(SPLIT, depth) // unit * unit // vocab_count
        self.rest = depth - self.wide * vocab_count
        self.both = self.rest // 2
        self.vocab_count = vocab_count

    def starts(self, v):
        return v * self.wide, self.wide * self.vocab_count + (v & 1) * self.both

    def spans(self, near):
        found = []
        for m in range(self.vocab_count):
            if (m < 2) == near:
                found.append((m, 0, self.wide, 0))
                if m < 2 and self.both:
                    found.append((m, self.wide, self.both, 1))
        return found


def sends(tok_count):
    if tok_count == 8:
        return [[1, 2], [4], [6, 3, 5], [7]]
    return [list(range(1, tok_count))]


def turns(tok_count):
    if tok_count == 8:
        return [[1, 2, 4, 3], [6, 5, 7]]
    return [list(range(1, tok_count))]


def gather_rows(hidden, targets, plan, tok_count, vocab_count):
    rows = hidden.shape[0]
    me = lax.axis_index("vocab")

    def move(value, mask):
        return hop(value, mask, tok_count * vocab_count)

    def own(v, full):
        one, two = plan.starts(v)
        parts = [lax.dynamic_slice_in_dim(hidden, one, plan.wide, axis=1)]
        if full and plan.both:
            parts.append(lax.dynamic_slice_in_dim(hidden, two, plan.both, axis=1))
        return parts

    first = with_ids(own(me, True), targets)
    along, across = {0: first}, {}
    step = tok_count // 4
    while step >= 1:
        along.update({k ^ step: move(along[k], step * 2 * vocab_count) for k in list(along)})
        step //= 2
    for k in along:
        across[k] = move(along[k], vocab_count)
    blocks = {2 * k: along[k] for k in along} | {2 * k + 1: across[k] for k in across}
    pieces = {0: [(blocks[b], 0, b) for b in blocks]}

    def joined(names, width):
        return jnp.concatenate([blocks[b][:, :width] for b in names], axis=0)

    for m in range(vocab_count):
        if m % 2:
            continue
        if m:
            pieces[m] = [(own(me ^ m, False)[0], 0, 0)]
            for names in sends(tok_count):
                got = move(joined(names, plan.wide), m)
                pieces[m] += [(got, i * rows, b) for i, b in enumerate(names)]
        pieces[m + 1] = [(jnp.concatenate(own(me ^ (m + 1), m == 0), axis=1), 0, 0)]
        if m == 0:
            groups = [(joined(names, plan.wide + plan.both), [(i * rows, b) for i, b in enumerate(names)]) for names in turns(tok_count)]
        else:
            seen = {}
            for array, at, b in pieces[m][1:]:
                seen.setdefault(id(array), (array, []))[1].append((at, b))
            groups = list(seen.values())
        for array, places in groups:
            got = move(array, 1)
            pieces[m + 1] += [(got, at, b) for at, b in places]
    return pieces


def chunked(spans):
    found, at = [], 0
    for m, _, width, kind in spans:
        for cut in range(0, width, CHUNK):
            part = min(CHUNK, width - cut)
            found.append((at, (m, kind), cut, part))
            at += part
    return found


def copies_of(cut_spans, plan, heads, stores, sems, low):
    found = []
    me = lax.axis_index("vocab")
    for i, (at, key, cut, part) in enumerate(cut_spans):
        for j, (head, store) in enumerate(zip(heads, stores)):
            start = plan.starts(me ^ key[0])[key[1]]
            src = pl.ds(pl.multiple_of(start, LANES) + cut, part)
            found.append(pltpu.make_async_copy(head.at[src, :], store.at[pl.ds(at - low, part), :], sems.at[i, j]))
    return found


def load_kernel(cuts, plan, policy_ref, reference_ref, stored, sems):
    copies = copies_of(cuts, plan, (policy_ref, reference_ref), [stored.at[0], stored.at[1]], sems, 0)
    for copy in copies:
        copy.start()
    for copy in copies:
        copy.wait()


def fill(layout, refs, rows, lhs):
    for index, row, column, width, block, to in layout:
        lhs[block * rows : (block + 1) * rows, to : to + width] = refs[index][row : row + rows, column : column + width]


def multiply(lhs, low, high, store, tile, put):
    @pl.loop(0, store.shape[1] // tile)
    def _(step):
        at = pl.ds(pl.multiple_of(step * tile, tile), tile)
        put(at, jnp.dot(lhs[:, low:high], store[0 : high - low, at], preferred_element_type=jnp.float32))


def partial_kernel(layout, count, rows, tile, *refs):
    blocks, stored, outs, lhs = refs[:count], refs[count], refs[count + 1 : count + 3], refs[count + 3]
    fill(layout, blocks, rows, lhs)
    for j, out in enumerate(outs):

        def put(at, value):
            out[:, at] = value

        multiply(lhs, 0, lhs.shape[1], stored.at[j], tile, put)


def last_kernel(layout, count, rows, tile, base, ahead, cuts, plan, ids, copies_each, *refs):
    blocks, stored, parts, heads = refs[:count], refs[count], refs[count + 1 : count + 3], refs[count + 3 : count + 5]
    out_ref, lhs, policy_ref, reference_ref, fresh, sems = refs[count + 5 :]
    logits = (policy_ref, reference_ref)
    columns = policy_ref.shape[1]
    copies = copies_of(cuts, plan, heads, [fresh.at[0], fresh.at[1]], sems, ahead)
    for copy in copies:
        copy.start()
    fill(layout, blocks, rows, lhs)
    if ahead:
        for j, (part, logit) in enumerate(zip(parts, logits)):

            def put(at, value):
                logit[:, at] = part[:, at] + value

            multiply(lhs, 0, ahead, stored.at[j, pl.ds(base, ahead)], tile, put)
    groups = 1 if ahead else 2
    size = -(-len(cuts) // groups)
    for i in range(0, len(cuts), size):
        low, high = cuts[i][0], cuts[i + size][0] if i + size < len(cuts) else lhs.shape[1]
        for j, (part, logit) in enumerate(zip(parts, logits)):
            for copy in copies[2 * i + j : 2 * (i + size) : 2]:
                copy.wait()

            def more(at, value):
                logit[:, at] = (logit if low else part)[:, at] + value

            multiply(lhs, low, high, fresh.at[j, pl.ds(low - ahead, high - low)], tile, more)

    digits = jnp.concatenate([blocks[i][row : row + rows, column : column + LANES] for i, row, column in ids], axis=0)
    digits = digits.astype(jnp.float32)
    ids = digits[:, 0:1] + digits[:, 1:2] * 256.0 + digits[:, 2:3] * 65536.0
    policy, reference = logits[0][...], logits[1][...]
    base = ((lax.axis_index("tok") * lax.axis_size("vocab") + lax.axis_index("vocab")) * columns).astype(jnp.float32)
    hits = lax.broadcasted_iota(jnp.int32, policy.shape, 1).astype(jnp.float32) == ids - base
    peak_policy = jnp.max(policy, axis=1, keepdims=True)
    peak_reference = jnp.max(reference, axis=1, keepdims=True)
    policy_exp = jnp.exp(policy - peak_policy)
    stats = (
        peak_policy,
        peak_reference,
        jnp.sum(policy_exp, axis=1, keepdims=True),
        jnp.sum(jnp.exp(reference - peak_reference), axis=1, keepdims=True),
        jnp.sum(policy_exp * (policy - reference), axis=1, keepdims=True),
        jnp.sum(jnp.where(hits, policy, 0.0), axis=1, keepdims=True),
        jnp.sum(jnp.where(hits, reference, 0.0), axis=1, keepdims=True),
    )
    lane = lax.broadcasted_iota(jnp.int32, (policy.shape[0], LANES), 1)
    table = jnp.zeros((policy.shape[0], LANES), jnp.float32)
    for s, stat in enumerate(stats):
        table = jnp.where(lane == s, stat, table)
    turned = table.T
    me = lax.axis_index("tok")
    for b in range(policy.shape[0] // rows):
        line = jnp.concatenate([turned[s : s + 1, b * rows : (b + 1) * rows] for s in range(STATS)], axis=1)
        spare = out_ref.shape[2] - STATS * rows
        line = jnp.concatenate([line, jnp.zeros((1, spare), jnp.float32)], axis=1)
        for j in range(copies_each):
            out_ref[(me ^ b) * copies_each + j] = line


def finish_kernel(rows, got_ref, policy_ref, reference_ref, divergence_ref):
    got = got_ref[...][:, 0, :]
    stat = [got[:, s * rows : (s + 1) * rows] for s in range(STATS)]
    peak_policy = jnp.max(stat[0], axis=0, keepdims=True)
    peak_reference = jnp.max(stat[1], axis=0, keepdims=True)
    policy_scale = jnp.exp(stat[0] - peak_policy)
    reference_scale = jnp.exp(stat[1] - peak_reference)
    total_policy = jnp.sum(stat[2] * policy_scale, axis=0, keepdims=True)
    total_reference = jnp.sum(stat[3] * reference_scale, axis=0, keepdims=True)
    weighted = jnp.sum(stat[4] * policy_scale, axis=0, keepdims=True)
    log_norm_policy = peak_policy + jnp.log(total_policy)
    log_norm_reference = peak_reference + jnp.log(total_reference)
    policy_ref[...] = jnp.sum(stat[5], axis=0, keepdims=True) - log_norm_policy
    reference_ref[...] = jnp.sum(stat[6], axis=0, keepdims=True) - log_norm_reference
    divergence_ref[...] = weighted / total_policy - log_norm_policy + log_norm_reference


def in_vmem(value):
    return pltpu.with_memory_space_constraint(value, pltpu.VMEM)


def layout_of(pieces, spans):
    arrays, layout, to = [], [], 0
    for m, column, width, _ in spans:
        for array, row, block in pieces[m]:
            index = next((i for i, seen in enumerate(arrays) if seen is array), len(arrays))
            if index == len(arrays):
                arrays.append(array)
            layout.append((index, row, column, width, block, to))
        to += width
    return arrays, layout, to


def body(hidden, policy_head, reference_head, targets):
    tok_count = lax.axis_size("tok")
    vocab_count = lax.axis_size("vocab")
    rows, depth = hidden.shape
    columns = policy_head.shape[1]
    tokens = rows * tok_count
    plan = Plan(depth, vocab_count)
    pieces = gather_rows(hidden, targets, plan, tok_count, vocab_count)
    vmem, hbm = (pl.BlockSpec(memory_space=space) for space in (pltpu.VMEM, pltpu.HBM))
    heads = [pltpu.with_memory_space_constraint(head, pltpu.HBM) for head in (policy_head, reference_head)]
    tile = min(TILE, columns)
    kind = policy_head.dtype
    bytes_of = lambda *shape: 2 * functools.reduce(lambda a, b: a * b, shape)

    def prepared(near):
        spans = plan.spans(near)
        return chunked(spans), *layout_of(pieces, spans)

    def cost(width, exps=0):
        return pl.CostEstimate(flops=4 * tokens * columns * width, bytes_accessed=0, transcendentals=exps)

    cuts, arrays, layout, width = prepared(True)
    far_cuts, far_arrays, far_layout, far_width = prepared(False)
    ahead = max([at + part for at, _, _, part in far_cuts if at + part <= AHEAD] or [0])
    soon = [(width + cut[0], *cut[1:]) for cut in far_cuts if cut[0] < ahead]
    later = [cut for cut in far_cuts if cut[0] >= ahead]
    left = far_width - ahead
    limit = pltpu.CompilerParams(
        vmem_limit_bytes=MARGIN + bytes_of(tokens, far_width) + bytes_of(4, tokens, columns) + bytes_of(2, left, columns)
    )
    stored = pl.pallas_call(
        functools.partial(load_kernel, cuts + soon, plan),
        out_shape=pltpu.VMEM((2, width + ahead, columns), kind),
        in_specs=[hbm] * 2,
        out_specs=vmem,
        scratch_shapes=[pltpu.SemaphoreType.DMA((len(cuts + soon), 2))],
        compiler_params=limit,
        cost_estimate=cost(width),
        name="load_first",
    )(*heads)

    parts = pl.pallas_call(
        functools.partial(partial_kernel, layout, len(arrays), rows, tile),
        out_shape=[pltpu.VMEM((tokens, columns), jnp.float32)] * 2,
        in_specs=[vmem] * (len(arrays) + 1),
        out_specs=[vmem] * 2,
        scratch_shapes=[pltpu.VMEM((tokens, width), kind)],
        compiler_params=limit,
        cost_estimate=cost(width),
        name="first_part",
    )(*[in_vmem(a) for a in arrays], in_vmem(stored))

    ids = {}
    for array, row, block in pieces[0]:
        index = next((i for i, seen in enumerate(far_arrays) if seen is array), len(far_arrays))
        if index == len(far_arrays):
            far_arrays.append(array)
        ids[block] = (index, row, plan.wide + plan.both)
    span = -(-STATS * rows // LANES) * LANES
    packed = pl.pallas_call(
        functools.partial(
            last_kernel, far_layout, len(far_arrays), rows, tile, width, ahead, later, plan,
            [ids[b] for b in range(tok_count)], vocab_count,
        ),
        out_shape=jax.ShapeDtypeStruct((tok_count * vocab_count, 1, span), jnp.float32),
        in_specs=[vmem] * (len(far_arrays) + 3) + [hbm] * 2,
        out_specs=vmem,
        scratch_shapes=[
            pltpu.VMEM((tokens, far_width), kind),
            pltpu.VMEM((tokens, columns), jnp.float32),
            pltpu.VMEM((tokens, columns), jnp.float32),
            pltpu.VMEM((2, left, columns), kind),
            pltpu.SemaphoreType.DMA((len(later), 2)),
        ],
        compiler_params=limit,
        cost_estimate=cost(far_width, 2 * tokens * columns),
        name="last_part",
    )(
        *[in_vmem(a) for a in far_arrays],
        in_vmem(stored),
        *[in_vmem(p) for p in parts],
        *heads,
    )

    got = lax.all_to_all(packed, ("tok", "vocab"), split_axis=0, concat_axis=0, tiled=True)
    outs = pl.pallas_call(
        functools.partial(finish_kernel, rows),
        out_shape=[jax.ShapeDtypeStruct((1, rows), jnp.float32)] * 3,
        in_specs=[vmem],
        out_specs=[vmem] * 3,
        name="finish",
    )(got)
    return tuple(out.reshape(rows) for out in outs)


def solution(mesh):
    in_specs = (P("tok", None), P(None, ("tok", "vocab")), P(None, ("tok", "vocab")), P("tok"))
    out_specs = (P("tok"), P("tok"), P("tok"))

    return jax.shard_map(body, mesh=mesh, in_specs=in_specs, out_specs=out_specs, check_vma=False)
```

time: 180 us -> 63.6 us (0.35)
  waiting for transfers between devices: 92.7 us -> 12.7 us
  Pallas kernels: 0 us -> 22.2 us
  matrix products: 15.6 us -> 0 us
  between operations: 15.5 us -> 0.81 us
  local copies, waits for them, and re-layouts: 12.7 us -> 1.25 us
  starting transfers between devices: 23.1 us -> 14.5 us
  blocking collectives: 18.7 us -> 11.1 us
    all_gather x1 -> x0, waiting for transfers between devices: 53.8 us -> none  [body(): piece = lax.all_gather(hidden, 'tok', axis=0, tiled=True)]
    all_to_all x7 -> x0, waiting for transfers between devices: 38.3 us -> none  [body(): lax.all_to_all(shaped, 'tok', split_axis=0, concat_axis=0, tiled=True)]
    all_to_all x7 -> x0, starting transfers between devices: 23 us -> none  [body(): lax.all_to_all(shaped, 'tok', split_axis=0, concat_axis=0, tiled=True)]
    pallas_call x0 -> x4, Pallas kernels: none -> 22.2 us  [the longest x1 9.66 us: body(): pl.pallas_call(functools.partial(last_kernel, far_layout, len(far_arrays)...]
    unnamed x2 -> x0, blocking collectives: 18.7 us -> none
    dot_general x2 -> x0, matrix products: 15.6 us -> none  [the longest x1 9.63 us: body(): jnp.dot(piece, policy_head, preferred_element_type=jnp.float32)]
    ppermute x0 -> x17, starting transfers between devices: none -> 14.5 us  [hop(): return lax.ppermute(value, ('tok', 'vocab'), pairs)]
    ppermute x0 -> x17, waiting for transfers between devices: none -> 12.7 us  [hop(): return lax.ppermute(value, ('tok', 'vocab'), pairs)]
  transfers between devices with their start and end apart: 8 -> 17, of which waited for: 8 -> 5; matrix products, arithmetic and copies ran while one was open for 2% -> 0% of each run, Pallas kernels for 0% -> 17%
where the time goes in v1:
time: 63.6 us; the launch traced here: 63.4 us
  Pallas kernels  22.2 us (35%)
  starting transfers between devices  14.5 us (23%)
  waiting for transfers between devices  12.7 us (20%)
  blocking collectives  11.1 us (17%)
  local copies, waits for them, and re-layouts  1.25 us (2%)
  between operations  0.81 us (1%)
  other arithmetic  0.78 us (1%)
    ppermute x17, starting transfers between devices, hop(): return lax.ppermute(value, ('tok', 'vocab'), pairs)  14.5 us
    ppermute x17, waiting for transfers between devices, hop(): return lax.ppermute(value, ('tok', 'vocab'), pairs)  12.7 us
    all_to_all x1, blocking collectives, body(): lax.all_to_all(packed, ('tok', 'vocab'), split_axis=0, concat_axis=0, til...  11.1 us
    pallas_call x1, Pallas kernels, body(): pl.pallas_call(functools.partial(last_kernel, far_layout, len(far_arrays)...  9.66 us
    pallas_call x1, Pallas kernels, body(): pl.pallas_call(functools.partial(load_kernel, cuts + soon, plan), out_sha...  6.52 us
    pallas_call x1, Pallas kernels, body(): pl.pallas_call(functools.partial(partial_kernel, layout, len(arrays), row...  4.49 us
    pallas_call x1, Pallas kernels, body(): pl.pallas_call(functools.partial(finish_kernel, rows), out_shape=[jax.Sha...  1.51 us
  transfers between devices with their start and end apart: 17, of which 5 were waited for; matrix products, arithmetic and copies ran while one was open for 0% of the time, Pallas kernels for 17%

profile of v1, /device:TPU:0, one launch (start us, length us, event | category | flops | bytes accessed | tf_op | source)
XLA Modules:
  0.0 63.4 jit_solution(6864006786003685640)
XLA Ops:
  0.6 0.7 %convert_bitcast_fusion.2 = (bf16[24,1]{0,1:T(2,128)(2,1)S(1)}, bf16[24,1]{0,1:T(2,128)(2,1)S(1)}, bf16[24,1]{0,1:T(2,128)(2,1)S(1)}) fusion(s32[24]{0:T(128)} %param.7), kind=kLoop, calls=%fused_computation.16 | loop fusion | flops 216 | bytes 240 | tf_op jit(solution)/shard_map/stack | solution.py:26
  1.3 0.1 copy.10
  1.4 1.1 %constant_dynamic-slice_fusion = (bf16[24,2304]{1,0:T(8,128)(2,1)S(1)}, bf16[24,2304]{1,0:T(8,128)(2,1)S(1)}, bf16[24,2304]{1,0:T(8,128)(2,1)S(1)}, bf16[24,2304]{1,0:T(8,128)(2,1)S(1)}) fusion(bf16[24,9216]{1,0:T(8,128)(2,1)} %param.4, s32[]{:T(128)S(6)} %select_n.15, s32[]{:T(128)S(6)} %select_n.13, s32[]{:T(128)S(6)} %select_n.12, s32[]{:T(128)S(6)} %select_n.14), kind=kLoop, calls=%fused_computation.10 | loop fusion | bytes 884752 | tf_op jit(solution)/shard_map/dynamic_slice | solution.py:73
  2.5 3.1 %collective-permute-start.1 = (bf16[24,2432]{1,0:T(8,128)(2,1)S(1)}, bf16[24,2432]{1,0:T(8,128)(2,1)S(1)}, u32[]{:S(2)}, u32[]{:S(2)}) collective-permute-start(bf16[24,2432]{1,0:T(8,128)(2,1)S(1)} %fusion.3.refs_0_.refs_10_), channel_id=1, source_target_pairs={{0,8},{1,9},{2,10},{3,11},{4,12},{5,13},{6,14},{7,15},{8,0},{9,1},... | collective-permute-start | bytes 350216 | tf_op jit(solution)/shard_map/ppermute | solution.py:22
  5.7 1.5 %collective-permute-start = (bf16[24,2432]{1,0:T(8,128)(2,1)S(1)}, bf16[24,2432]{1,0:T(8,128)(2,1)S(1)}, u32[]{:S(2)}, u32[]{:S(2)}) collective-permute-start(bf16[24,2432]{1,0:T(8,128)(2,1)S(1)} %fusion.3.refs_0_.refs_10_), channel_id=1, source_target_pairs={{0,4},{1,5},{2,6},{3,7},{4,0},{5,1},{6,2},{7,3},{8,12},{9,13},{10,... | collective-permute-start | bytes 350216 | tf_op jit(solution)/shard_map/ppermute | solution.py:22
  7.2 2.6 %collective-permute-start.3 = (bf16[24,2432]{1,0:T(8,128)(2,1)S(1)}, bf16[24,2432]{1,0:T(8,128)(2,1)S(1)}, u32[]{:S(2)}, u32[]{:S(2)}) collective-permute-start(bf16[24,2432]{1,0:T(8,128)(2,1)S(1)} %fusion.3.refs_0_.refs_10_), channel_id=1, source_target_pairs={{0,16},{1,17},{2,18},{3,19},{4,20},{5,21},{6,22},{7,23},{8,24},{9,... | collective-permute-start | bytes 350216 | tf_op jit(solution)/shard_map/ppermute | solution.py:22
  9.8 0.0 collective-permute-done.1.refs_2_.refs_12_
  9.8 0.8 %collective-permute-start.6 = (bf16[24,2432]{1,0:T(8,128)(2,1)S(1)}, bf16[24,2432]{1,0:T(8,128)(2,1)S(1)}, u32[]{:S(2)}, u32[]{:S(2)}) collective-permute-start(bf16[24,2432]{1,0:T(8,128)(2,1)S(1)} %collective-permute-done.1.refs_2_.refs_12_), channel_id=1, source_target_pairs={{0,4},{1,5},{2,6},{3,7},{4,0},{5,1},{6,2},{7,3},{8,12},{9,13},{10,... | collective-permute-start | bytes 350216 | tf_op jit(solution)/shard_map/ppermute | solution.py:22
  10.5 0.0 collective-permute-done.refs_4_.refs_14_
  10.6 4.3 %collective-permute-done.3.refs_1_.refs_11_ = bf16[24,2432]{1,0:T(8,128)(2,1)S(1)} collective-permute-done((bf16[24,2432]{1,0:T(8,128)(2,1)S(1)}, bf16[24,2432]{1,0:T(8,128)(2,1)S(1)}, u32[]{:S(2)}, u32[]{:S(2)}) %collective-permute-start.3) | collective-permute-done | bytes 116768 | tf_op jit(solution)/shard_map/ppermute | solution.py:22
  14.9 0.0 collective-permute-start.5
  14.9 1.6 %collective-permute-start.2 = (bf16[48,2304]{1,0:T(8,128)(2,1)S(1)}, bf16[48,2304]{1,0:T(8,128)(2,1)S(1)}, u32[]{:S(2)}, u32[]{:S(2)}) collective-permute-start(bf16[48,2304]{1,0:T(8,128)(2,1)S(1)} %pad_maximum_fusion.3), channel_id=1, source_target_pairs={{0,2},{1,3},{2,0},{3,1},{4,6},{5,7},{6,4},{7,5},{8,10},{9,11},{10,... | collective-permute-start | bytes 663560 | tf_op jit(solution)/shard_map/ppermute | solution.py:22
  16.5 0.6 collective-permute-start.4
  17.1 0.7 %collective-permute-start.7 = (bf16[24,2432]{1,0:T(8,128)(2,1)S(1)}, bf16[24,2432]{1,0:T(8,128)(2,1)S(1)}, u32[]{:S(2)}, u32[]{:S(2)}) collective-permute-start(bf16[24,2432]{1,0:T(8,128)(2,1)S(1)} %collective-permute-done.3.refs_1_.refs_11_), channel_id=1, source_target_pairs={{0,4},{1,5},{2,6},{3,7},{4,0},{5,1},{6,2},{7,3},{8,12},{9,13},{10,... | collective-permute-start | bytes 350216 | tf_op jit(solution)/shard_map/ppermute | solution.py:22
  17.8 0.0 collective-permute-done.6.refs_6_.refs_16_
  17.8 1.9 %collective-permute-done.5.refs_3_.refs_13_ = bf16[24,2432]{1,0:T(8,128)(2,1)S(1)} collective-permute-done((bf16[24,2432]{1,0:T(8,128)(2,1)S(1)}, bf16[24,2432]{1,0:T(8,128)(2,1)S(1)}, u32[]{:S(2)}, u32[]{:S(2)}) %collective-permute-start.5) | collective-permute-done | bytes 116768 | tf_op jit(solution)/shard_map/ppermute | solution.py:22
  19.7 0.6 collective-permute-start.9
  20.4 0.1 collective-permute-start.15
  20.5 2.5 %collective-permute-done.7.refs_5_.refs_15_ = bf16[24,2432]{1,0:T(8,128)(2,1)S(1)} collective-permute-done((bf16[24,2432]{1,0:T(8,128)(2,1)S(1)}, bf16[24,2432]{1,0:T(8,128)(2,1)S(1)}, u32[]{:S(2)}, u32[]{:S(2)}) %collective-permute-start.7) | collective-permute-done | bytes 116768 | tf_op jit(solution)/shard_map/ppermute | solution.py:22
  23.0 1.6 %collective-permute-done.9.refs_7_.refs_17_ = bf16[24,2432]{1,0:T(8,128)(2,1)S(1)} collective-permute-done((bf16[24,2432]{1,0:T(8,128)(2,1)S(1)}, bf16[24,2432]{1,0:T(8,128)(2,1)S(1)}, u32[]{:S(2)}, u32[]{:S(2)}) %collective-permute-start.9) | collective-permute-done | bytes 116768 | tf_op jit(solution)/shard_map/ppermute | solution.py:22
  24.6 1.6 %collective-permute-start.10 = (bf16[24,2304]{1,0:T(8,128)(2,1)S(1)}, bf16[24,2304]{1,0:T(8,128)(2,1)S(1)}, u32[]{:S(2)}, u32[]{:S(2)}) collective-permute-start(bf16[24,2304]{1,0:T(8,128)(2,1)S(1)} %slice.41), channel_id=1, source_target_pairs={{0,2},{1,3},{2,0},{3,1},{4,6},{5,7},{6,4},{7,5},{8,10},{9,11},{10,... | collective-permute-start | bytes 331784 | tf_op jit(solution)/shard_map/ppermute | solution.py:22
  26.2 0.1 collective-permute-start.16
  26.2 0.0 collective-permute-done.4.refs_2_
  26.3 0.6 collective-permute-start.8
  26.9 6.5 %load_first.1.refs_11_.refs_18_ = bf16[2,4608,1024]{2,1,0:T(8,128)(2,1)S(1)} custom-call(bf16[9216,1024]{1,0:T(8,128)(2,1)} %refs_21_.1, bf16[9216,1024]{1,0:T(8,128)(2,1)} %refs_22_.1), custom_call_target="tpu_custom_call" | custom-call | flops 3623878656 | tf_op jit(solution)/shard_map/load_first/pallas_call | solution.py:290
  33.4 0.0 collective-permute-done.2.refs_1_
  33.4 0.2 collective-permute-start.12
  33.6 0.0 collective-permute-done.10.refs_4_
  33.6 0.4 collective-permute-start.11
  34.0 0.0 collective-permute-done.15.refs_9_
  34.0 0.1 collective-permute-start.14
  34.1 2.4 %collective-permute-done.8.refs_3_ = bf16[72,2304]{1,0:T(8,128)(2,1)S(1)} collective-permute-done((bf16[72,2304]{1,0:T(8,128)(2,1)S(1)}, bf16[72,2304]{1,0:T(8,128)(2,1)S(1)}, u32[]{:S(2)}, u32[]{:S(2)}) %collective-permute-start.8) | collective-permute-done | bytes 331808 | tf_op jit(solution)/shard_map/ppermute | solution.py:22
  36.5 0.0 collective-permute-start.13
  36.5 0.0 collective-permute-done.16.refs_10_
  36.5 4.5 %first_part.1 = (f32[192,1024]{1,0:T(8,128)S(1)}, f32[192,1024]{1,0:T(8,128)S(1)}) custom-call(bf16[24,2432]{1,0:T(8,128)(2,1)S(1)} %fusion.3.refs_0_.refs_10_, bf16[24,2432]{1,0:T(8,128)(2,1)S(1)} %collective-permute-done.3.refs_1_.refs_11_, bf16[24,2432]{1,0:T(8,128)(2,1)S(1)} %collective-permute-done.1.refs_2_.refs_12_, ...), custom_call_target="tpu_custom_call" | custom-call | flops 3623878656 | tf_op jit(solution)/shard_map/first_part/pallas_call | solution.py:301
  41.0 0.0 collective-permute-done.12.refs_7_
  41.0 0.0 collective-permute-done.11.refs_6_
  41.0 0.0 collective-permute-done.14.refs_9_
  41.0 0.0 collective-permute-done.13.refs_8_
  41.0 9.7 %last_part.1 = f32[32,1,256]{2,1,0:T(1,128)S(1)} custom-call(bf16[24,2304]{1,0:T(8,128)(2,1)S(1)} %get-tuple-element.15.refs_0_, bf16[48,2304]{1,0:T(8,128)(2,1)S(1)} %collective-permute-done.2.refs_1_, bf16[24,2304]{1,0:T(8,128)(2,1)S(1)} %collective-permute-done.4.refs_2_, bf16[72,2304]{1,0:T(8,128)(2,1)S(1)} %collective-permute-done.8.refs_3_, ...), custom_call_target="tpu_custom_call" | custom-call | flops 3623878656 | tf_op jit(solution)/shard_map/last_part/pallas_call | solution.py:319
  50.7 11.1 %all_to_all.5.got_ref = f32[32,1,256]{2,1,0:T(1,128)} all-to-all(f32[32,1,256]{2,1,0:T(1,128)S(1)} %last_part.1), channel_id=1, replica_groups=mesh['tok'=8,'vocab'=4] {'tok','vocab'}, dimensions={0} | all-to-all | bytes 65536 | tf_op jit(solution)/shard_map/all_to_all | solution.py:344
  61.8 1.5 %finish.1 = (f32[1,24]{1,0:T(1,128)}, f32[1,24]{1,0:T(1,128)}, f32[1,24]{1,0:T(1,128)}) custom-call(f32[32,1,256]{2,1,0:T(1,128)} %all_to_all.5.got_ref), custom_call_target="tpu_custom_call" | custom-call | tf_op jit(solution)/shard_map/finish/pallas_call | solution.py:345
  (12 shorter events, 0.2 us)
Async XLA Ops:
  2.5 7.2 %collective-permute-start.1 = (bf16[24,2432]{1,0:T(8,128)(2,1)S(1)}, bf16[24,2432]{1,0:T(8,128)(2,1)S(1)}, u32[]{:S(2)}, u32[]{:S(2)}) collective-permute-start(bf16[24,2432]{1,0:T(8,128)(2,1)S(1)} %fusion.3.refs_0_.refs_10_), channel_id=1, source_target_pairs={{0,8},{1,9},{2,10},{3,11},{4,12},{5,13},{6,14},{7,15},{8,0},{9,1},... | collective-permute-start | bytes 350216 | tf_op jit(solution)/shard_map/ppermute | solution.py:22
  5.7 4.9 %collective-permute-start = (bf16[24,2432]{1,0:T(8,128)(2,1)S(1)}, bf16[24,2432]{1,0:T(8,128)(2,1)S(1)}, u32[]{:S(2)}, u32[]{:S(2)}) collective-permute-start(bf16[24,2432]{1,0:T(8,128)(2,1)S(1)} %fusion.3.refs_0_.refs_10_), channel_id=1, source_target_pairs={{0,4},{1,5},{2,6},{3,7},{4,0},{5,1},{6,2},{7,3},{8,12},{9,13},{10,... | collective-permute-start | bytes 350216 | tf_op jit(solution)/shard_map/ppermute | solution.py:22
  7.2 7.7 %collective-permute-start.3 = (bf16[24,2432]{1,0:T(8,128)(2,1)S(1)}, bf16[24,2432]{1,0:T(8,128)(2,1)S(1)}, u32[]{:S(2)}, u32[]{:S(2)}) collective-permute-start(bf16[24,2432]{1,0:T(8,128)(2,1)S(1)} %fusion.3.refs_0_.refs_10_), channel_id=1, source_target_pairs={{0,16},{1,17},{2,18},{3,19},{4,20},{5,21},{6,22},{7,23},{8,24},{9,... | collective-permute-start | bytes 350216 | tf_op jit(solution)/shard_map/ppermute | solution.py:22
  9.8 8.0 %collective-permute-start.6 = (bf16[24,2432]{1,0:T(8,128)(2,1)S(1)}, bf16[24,2432]{1,0:T(8,128)(2,1)S(1)}, u32[]{:S(2)}, u32[]{:S(2)}) collective-permute-start(bf16[24,2432]{1,0:T(8,128)(2,1)S(1)} %collective-permute-done.1.refs_2_.refs_12_), channel_id=1, source_target_pairs={{0,4},{1,5},{2,6},{3,7},{4,0},{5,1},{6,2},{7,3},{8,12},{9,13},{10,... | collective-permute-start | bytes 350216 | tf_op jit(solution)/shard_map/ppermute | solution.py:22
  14.9 4.8 %collective-permute-start.5 = (bf16[24,2432]{1,0:T(8,128)(2,1)S(1)}, bf16[24,2432]{1,0:T(8,128)(2,1)S(1)}, u32[]{:S(2)}, u32[]{:S(2)}) collective-permute-start(bf16[24,2432]{1,0:T(8,128)(2,1)S(1)} %collective-permute-done.3.refs_1_.refs_11_), channel_id=1, source_target_pairs={{0,8},{1,9},{2,10},{3,11},{4,12},{5,13},{6,14},{7,15},{8,0},{9,1},... | collective-permute-start | bytes 350216 | tf_op jit(solution)/shard_map/ppermute | solution.py:22
  14.9 18.4 %collective-permute-start.2 = (bf16[48,2304]{1,0:T(8,128)(2,1)S(1)}, bf16[48,2304]{1,0:T(8,128)(2,1)S(1)}, u32[]{:S(2)}, u32[]{:S(2)}) collective-permute-start(bf16[48,2304]{1,0:T(8,128)(2,1)S(1)} %pad_maximum_fusion.3), channel_id=1, source_target_pairs={{0,2},{1,3},{2,0},{3,1},{4,6},{5,7},{6,4},{7,5},{8,10},{9,11},{10,... | collective-permute-start | bytes 663560 | tf_op jit(solution)/shard_map/ppermute | solution.py:22
  16.5 9.7 %collective-permute-start.4 = (bf16[24,2304]{1,0:T(8,128)(2,1)S(1)}, bf16[24,2304]{1,0:T(8,128)(2,1)S(1)}, u32[]{:S(2)}, u32[]{:S(2)}) collective-permute-start(bf16[24,2304]{1,0:T(8,128)(2,1)S(1)} %slice.37), channel_id=1, source_target_pairs={{0,2},{1,3},{2,0},{3,1},{4,6},{5,7},{6,4},{7,5},{8,10},{9,11},{10,... | collective-permute-start | bytes 331784 | tf_op jit(solution)/shard_map/ppermute | solution.py:22
  17.1 5.8 %collective-permute-start.7 = (bf16[24,2432]{1,0:T(8,128)(2,1)S(1)}, bf16[24,2432]{1,0:T(8,128)(2,1)S(1)}, u32[]{:S(2)}, u32[]{:S(2)}) collective-permute-start(bf16[24,2432]{1,0:T(8,128)(2,1)S(1)} %collective-permute-done.3.refs_1_.refs_11_), channel_id=1, source_target_pairs={{0,4},{1,5},{2,6},{3,7},{4,0},{5,1},{6,2},{7,3},{8,12},{9,13},{10,... | collective-permute-start | bytes 350216 | tf_op jit(solution)/shard_map/ppermute | solution.py:22
  19.7 4.8 %collective-permute-start.9 = (bf16[24,2432]{1,0:T(8,128)(2,1)S(1)}, bf16[24,2432]{1,0:T(8,128)(2,1)S(1)}, u32[]{:S(2)}, u32[]{:S(2)}) collective-permute-start(bf16[24,2432]{1,0:T(8,128)(2,1)S(1)} %collective-permute-done.5.refs_3_.refs_13_), channel_id=1, source_target_pairs={{0,4},{1,5},{2,6},{3,7},{4,0},{5,1},{6,2},{7,3},{8,12},{9,13},{10,... | collective-permute-start | bytes 350216 | tf_op jit(solution)/shard_map/ppermute | solution.py:22
  20.4 13.6 %collective-permute-start.15 = (bf16[96,2304]{1,0:T(8,128)(2,1)S(1)}, bf16[96,2304]{1,0:T(8,128)(2,1)S(1)}, u32[]{:S(2)}, u32[]{:S(2)}) collective-permute-start(bf16[96,2304]{1,0:T(8,128)(2,1)S(1)} %pad_maximum_fusion), channel_id=1, source_target_pairs={{0,1},{1,0},{2,3},{3,2},{4,5},{5,4},{6,7},{7,6},{8,9},{9,8},{10,11... | collective-permute-start | bytes 1327112 | tf_op jit(solution)/shard_map/ppermute | solution.py:22
  24.6 9.0 %collective-permute-start.10 = (bf16[24,2304]{1,0:T(8,128)(2,1)S(1)}, bf16[24,2304]{1,0:T(8,128)(2,1)S(1)}, u32[]{:S(2)}, u32[]{:S(2)}) collective-permute-start(bf16[24,2304]{1,0:T(8,128)(2,1)S(1)} %slice.41), channel_id=1, source_target_pairs={{0,2},{1,3},{2,0},{3,1},{4,6},{5,7},{6,4},{7,5},{8,10},{9,11},{10,... | collective-permute-start | bytes 331784 | tf_op jit(solution)/shard_map/ppermute | solution.py:22
  26.2 10.3 %collective-permute-start.16 = (bf16[72,2304]{1,0:T(8,128)(2,1)S(1)}, bf16[72,2304]{1,0:T(8,128)(2,1)S(1)}, u32[]{:S(2)}, u32[]{:S(2)}) collective-permute-start(bf16[72,2304]{1,0:T(8,128)(2,1)S(1)} %get-tuple-element.17), channel_id=1, source_target_pairs={{0,1},{1,0},{2,3},{3,2},{4,5},{5,4},{6,7},{7,6},{8,9},{9,8},{10,11... | collective-permute-start | bytes 995336 | tf_op jit(solution)/shard_map/ppermute | solution.py:22
  26.3 10.2 %collective-permute-start.8 = (bf16[72,2304]{1,0:T(8,128)(2,1)S(1)}, bf16[72,2304]{1,0:T(8,128)(2,1)S(1)}, u32[]{:S(2)}, u32[]{:S(2)}) collective-permute-start(bf16[72,2304]{1,0:T(8,128)(2,1)S(1)} %get-tuple-element.18), channel_id=1, source_target_pairs={{0,2},{1,3},{2,0},{3,1},{4,6},{5,7},{6,4},{7,5},{8,10},{9,11},{10,... | collective-permute-start | bytes 995336 | tf_op jit(solution)/shard_map/ppermute | solution.py:22
  33.4 7.6 %collective-permute-start.12 = (bf16[24,2304]{1,0:T(8,128)(2,1)S(1)}, bf16[24,2304]{1,0:T(8,128)(2,1)S(1)}, u32[]{:S(2)}, u32[]{:S(2)}) collective-permute-start(bf16[24,2304]{1,0:T(8,128)(2,1)S(1)} %collective-permute-done.4.refs_2_), channel_id=1, source_target_pairs={{0,1},{1,0},{2,3},{3,2},{4,5},{5,4},{6,7},{7,6},{8,9},{9,8},{10,11... | collective-permute-start | bytes 331784 | tf_op jit(solution)/shard_map/ppermute | solution.py:22
  33.6 7.4 %collective-permute-start.11 = (bf16[48,2304]{1,0:T(8,128)(2,1)S(1)}, bf16[48,2304]{1,0:T(8,128)(2,1)S(1)}, u32[]{:S(2)}, u32[]{:S(2)}) collective-permute-start(bf16[48,2304]{1,0:T(8,128)(2,1)S(1)} %collective-permute-done.2.refs_1_), channel_id=1, source_target_pairs={{0,1},{1,0},{2,3},{3,2},{4,5},{5,4},{6,7},{7,6},{8,9},{9,8},{10,11... | collective-permute-start | bytes 663560 | tf_op jit(solution)/shard_map/ppermute | solution.py:22
  34.0 7.0 %collective-permute-start.14 = (bf16[24,2304]{1,0:T(8,128)(2,1)S(1)}, bf16[24,2304]{1,0:T(8,128)(2,1)S(1)}, u32[]{:S(2)}, u32[]{:S(2)}) collective-permute-start(bf16[24,2304]{1,0:T(8,128)(2,1)S(1)} %collective-permute-done.10.refs_4_), channel_id=1, source_target_pairs={{0,1},{1,0},{2,3},{3,2},{4,5},{5,4},{6,7},{7,6},{8,9},{9,8},{10,11... | collective-permute-start | bytes 331784 | tf_op jit(solution)/shard_map/ppermute | solution.py:22
  36.5 4.5 %collective-permute-start.13 = (bf16[72,2304]{1,0:T(8,128)(2,1)S(1)}, bf16[72,2304]{1,0:T(8,128)(2,1)S(1)}, u32[]{:S(2)}, u32[]{:S(2)}) collective-permute-start(bf16[72,2304]{1,0:T(8,128)(2,1)S(1)} %collective-permute-done.8.refs_3_), channel_id=1, source_target_pairs={{0,1},{1,0},{2,3},{3,2},{4,5},{5,4},{6,7},{7,6},{8,9},{9,8},{10,11... | collective-permute-start | bytes 995336 | tf_op jit(solution)/shard_map/ppermute | solution.py:22

commit v2 on v1

--- a/solution.py
+++ b/solution.py
@@ -13,7 +13,8 @@
 CHUNK = 768
 STATS = 7
 SPLIT = 9216
-AHEAD = 0
+AHEAD = 2304
+LOADS = (3072,)
 MARGIN = 4 << 20
 
 
@@ -22,10 +23,49 @@
     return lax.ppermute(value, ("tok", "vocab"), pairs)
 
 
-def with_ids(columns, targets):
-    digits = jnp.stack([(targets >> (8 * k)) & 255 for k in range(3)], axis=1)
-    digits = jnp.pad(digits, ((0, 0), (0, LANES - 3)))
-    return jnp.concatenate(columns + [digits.astype(columns[0].dtype)], axis=1)
+def own_kernel(plan, edges, hidden_ref, targets_ref, out_ref, targets_vmem, sems):
+    me = lax.axis_index("vocab")
+    fetch = pltpu.make_async_copy(targets_ref, targets_vmem, sems.at[2 * plan.vocab_count])
+    fetch.start()
+    copies = []
+    for m in range(plan.vocab_count):
+        for kind, (to, width) in enumerate(((0, plan.wide), (plan.wide, plan.both if m < 2 else 0))):
+            if width:
+                start = pl.multiple_of(plan.starts(me ^ m)[kind], LANES)
+                copies.append(
+                    pltpu.make_async_copy(
+                        hidden_ref.at[:, pl.ds(start, width)], out_ref.at[:, pl.ds(edges[m] + to, width)], sems.at[len(copies)]
+                    )
+                )
+    for copy in copies:
+        copy.start()
+    rows = hidden_ref.shape[0]
+    fetch.wait()
+    spread = jnp.broadcast_to(targets_vmem[...].astype(jnp.float32), (rows, rows))
+    here = lax.broadcasted_iota(jnp.int32, (rows, rows), 0) == lax.broadcasted_iota(jnp.int32, (rows, rows), 1)
+    ids = jnp.sum(jnp.where(here, spread, 0.0), axis=1, keepdims=True).astype(jnp.int32)
+    lane = lax.broadcasted_iota(jnp.int32, (rows, LANES), 1)
+    digits = jnp.where(lane < 3, (ids >> (8 * jnp.minimum(lane, 3))) & 255, 0)
+    out_ref[:, edges[1] - LANES : edges[1]] = digits.astype(jnp.float32).astype(out_ref.dtype)
+    for copy in copies:
+        copy.wait()
+
+
+def own_columns(hidden, targets, plan):
+    rows, kind = hidden.shape[0], hidden.dtype
+    widths = [plan.wide + (plan.both if m < 2 else 0) + (LANES if m == 0 else 0) for m in range(plan.vocab_count)]
+    edges = [sum(widths[:m]) for m in range(plan.vocab_count + 1)]
+    vmem, hbm = (pl.BlockSpec(memory_space=space) for space in (pltpu.VMEM, pltpu.HBM))
+    ordered = pl.pallas_call(
+        functools.partial(own_kernel, plan, edges),
+        out_shape=jax.ShapeDtypeStruct((rows, edges[-1]), kind),
+        in_specs=[hbm] * 2,
+        out_specs=vmem,
+        scratch_shapes=[pltpu.VMEM((1, rows), targets.dtype), pltpu.SemaphoreType.DMA((2 * plan.vocab_count + 1,))],
+        compiler_params=pltpu.CompilerParams(vmem_limit_bytes=MARGIN),
+        name="own_columns",
+    )(*[pltpu.with_memory_space_constraint(value, pltpu.HBM) for value in (hidden, targets.reshape(1, rows))])
+    return [ordered[:, low:high] for low, high in zip(edges, edges[1:])]
 
 
 class Plan:
@@ -63,19 +103,12 @@
 
 def gather_rows(hidden, targets, plan, tok_count, vocab_count):
     rows = hidden.shape[0]
-    me = lax.axis_index("vocab")
 
     def move(value, mask):
         return hop(value, mask, tok_count * vocab_count)
 
-    def own(v, full):
-        one, two = plan.starts(v)
-        parts = [lax.dynamic_slice_in_dim(hidden, one, plan.wide, axis=1)]
-        if full and plan.both:
-            parts.append(lax.dynamic_slice_in_dim(hidden, two, plan.both, axis=1))
-        return parts
-
-    first = with_ids(own(me, True), targets)
+    own = own_columns(hidden, targets, plan)
+    first = own[0]
     along, across = {0: first}, {}
     step = tok_count // 4
     while step >= 1:
@@ -87,17 +120,17 @@
     pieces = {0: [(blocks[b], 0, b) for b in blocks]}
 
     def joined(names, width):
-        return jnp.concatenate([blocks[b][:, :width] for b in names], axis=0)
+        return jnp.concatenate(lax.optimization_barrier([blocks[b][:, :width] for b in names]), axis=0)
 
     for m in range(vocab_count):
         if m % 2:
             continue
         if m:
-            pieces[m] = [(own(me ^ m, False)[0], 0, 0)]
+            pieces[m] = [(own[m], 0, 0)]
             for names in sends(tok_count):
                 got = move(joined(names, plan.wide), m)
                 pieces[m] += [(got, i * rows, b) for i, b in enumerate(names)]
-        pieces[m + 1] = [(jnp.concatenate(own(me ^ (m + 1), m == 0), axis=1), 0, 0)]
+        pieces[m + 1] = [(own[m + 1], 0, 0)]
         if m == 0:
             groups = [(joined(names, plan.wide + plan.both), [(i * rows, b) for i, b in enumerate(names)]) for names in turns(tok_count)]
         else:
@@ -132,7 +165,8 @@
     return found
 
 
-def load_kernel(cuts, plan, policy_ref, reference_ref, stored, sems):
+def load_kernel(cuts, plan, policy_ref, reference_ref, *refs):
+    stored, sems = refs[-2:]
     copies = copies_of(cuts, plan, (policy_ref, reference_ref), [stored.at[0], stored.at[1]], sems, 0)
     for copy in copies:
         copy.start()
@@ -152,15 +186,22 @@
         put(at, jnp.dot(lhs[:, low:high], store[0 : high - low, at], preferred_element_type=jnp.float32))
 
 
-def partial_kernel(layout, count, rows, tile, *refs):
-    blocks, stored, outs, lhs = refs[:count], refs[count], refs[count + 1 : count + 3], refs[count + 3]
+def partial_kernel(layout, count, rows, tile, cuts, plan, *refs):
+    heads, blocks, outs = refs[1:3], refs[3 : count + 3], refs[count + 3 : count + 5]
+    stored, lhs, sems = refs[count + 5 :]
+    copies = copies_of(cuts, plan, heads, [stored.at[0], stored.at[1]], sems, 0)
+    for copy in copies:
+        copy.start()
     fill(layout, blocks, rows, lhs)
+    width = lhs.shape[1]
     for j, out in enumerate(outs):
 
         def put(at, value):
             out[:, at] = value
 
-        multiply(lhs, 0, lhs.shape[1], stored.at[j], tile, put)
+        multiply(lhs, 0, width, stored.at[j, pl.ds(0, width)], tile, put)
+    for copy in copies:
+        copy.wait()
 
 
 def last_kernel(layout, count, rows, tile, base, ahead, cuts, plan, ids, copies_each, *refs):
@@ -169,7 +210,7 @@
     logits = (policy_ref, reference_ref)
     columns = policy_ref.shape[1]
     copies = copies_of(cuts, plan, heads, [fresh.at[0], fresh.at[1]], sems, ahead)
-    for copy in copies:
+    for copy in copies[0::2] + copies[1::2]:
         copy.start()
     fill(layout, blocks, rows, lhs)
     if ahead:
@@ -287,27 +328,34 @@
     limit = pltpu.CompilerParams(
         vmem_limit_bytes=MARGIN + bytes_of(tokens, far_width) + bytes_of(4, tokens, columns) + bytes_of(2, left, columns)
     )
-    stored = pl.pallas_call(
-        functools.partial(load_kernel, cuts + soon, plan),
-        out_shape=pltpu.VMEM((2, width + ahead, columns), kind),
-        in_specs=[hbm] * 2,
-        out_specs=vmem,
-        scratch_shapes=[pltpu.SemaphoreType.DMA((len(cuts + soon), 2))],
-        compiler_params=limit,
-        cost_estimate=cost(width),
-        name="load_first",
-    )(*heads)
-
-    parts = pl.pallas_call(
-        functools.partial(partial_kernel, layout, len(arrays), rows, tile),
-        out_shape=[pltpu.VMEM((tokens, columns), jnp.float32)] * 2,
-        in_specs=[vmem] * (len(arrays) + 1),
-        out_specs=[vmem] * 2,
-        scratch_shapes=[pltpu.VMEM((tokens, width), kind)],
+    store = pltpu.VMEM((2, width + ahead, columns), kind)
+    limits = [at for at in LOADS if at < width] + [width]
+    stored = None
+    for i, (low, high) in enumerate(zip([0] + limits, limits)):
+        part = [cut for cut in cuts if low <= cut[0] < high]
+        stored = pl.pallas_call(
+            functools.partial(load_kernel, part, plan),
+            out_shape=store,
+            in_specs=[hbm] * 2 + [vmem] * (i > 0),
+            out_specs=vmem,
+            scratch_shapes=[pltpu.SemaphoreType.DMA((len(part), 2))],
+            input_output_aliases={2: 0} if i else {},
+            compiler_params=limit,
+            cost_estimate=cost(high - low),
+            name="load_heads",
+        )(*heads, *([in_vmem(stored)] if i else []))
+
+    *parts, stored = pl.pallas_call(
+        functools.partial(partial_kernel, layout, len(arrays), rows, tile, soon, plan),
+        out_shape=[pltpu.VMEM((tokens, columns), jnp.float32)] * 2 + [store],
+        in_specs=[vmem] + [hbm] * 2 + [vmem] * len(arrays),
+        out_specs=[vmem] * 3,
+        scratch_shapes=[pltpu.VMEM((tokens, width), kind), pltpu.SemaphoreType.DMA((len(soon) or 1, 2))],
+        input_output_aliases={0: 2},
         compiler_params=limit,
         cost_estimate=cost(width),
         name="first_part",
-    )(*[in_vmem(a) for a in arrays], in_vmem(stored))
+    )(in_vmem(stored), *heads, *[in_vmem(a) for a in arrays])
 
     ids = {}
     for array, row, block in pieces[0]:
@@ -348,7 +396,7 @@
         in_specs=[vmem],
         out_specs=[vmem] * 3,
         name="finish",
-    )(got)
+    )(in_vmem(got))
     return tuple(out.reshape(rows) for out in outs)
 
 

time: 63.6 us -> 60 us (0.943)
  starting transfers between devices: 14.5 us -> 16.5 us
  waiting for transfers between devices: 12.7 us -> 11 us
  Pallas kernels: 22.2 us -> 20.6 us
  local copies, waits for them, and re-layouts: 1.25 us -> 0.09 us
  other arithmetic: 0.78 us -> 0.1 us
    pallas_call x1, Pallas kernels: 9.66 us -> 6.37 us  [body(): pl.pallas_call(functools.partial(last_kernel, far_layout, len(far_arrays)...]
    pallas_call x1 -> x3, Pallas kernels: 6.52 us -> 8.83 us  [the longest x2 7.68 us: body(): pl.pallas_call(functools.partial(load_kernel, part, plan), out_shape=stor...]
    ppermute x17, starting transfers between devices: 14.5 us -> 16.5 us  [hop(): return lax.ppermute(value, ('tok', 'vocab'), pairs)]
    ppermute x17, waiting for transfers between devices: 12.7 us -> 11 us  [hop(): return lax.ppermute(value, ('tok', 'vocab'), pairs)]
    dynamic_slice x1 -> x0, local copies, waits for them, and re-layouts: 1.09 us -> none  [own(): parts = [lax.dynamic_slice_in_dim(hidden, one, plan.wide, axis=1)]]
    pallas_call x1, Pallas kernels: 1.51 us -> 0.75 us  [body(): pl.pallas_call(functools.partial(finish_kernel, rows), out_shape=[jax.Sha...]
    another operation x2 -> x0, other arithmetic: 0.67 us -> none  [with_ids(): digits = jnp.stack([targets >> 8 * k & 255 for k in range(3)], axis=1)]
  transfers between devices with their start and end apart: 17 -> 17, of which waited for: 5 -> 7; matrix products, arithmetic and copies ran while one was open for 0% -> 0% of each run, Pallas kernels for 17% -> 21%
where the time goes in v2:
time: 60 us; the launch traced here: 59.9 us
  Pallas kernels  20.6 us (34%)
  starting transfers between devices  16.5 us (28%)
  waiting for transfers between devices  11 us (18%)
  blocking collectives  10.8 us (18%)
  between operations  0.81 us (1%)
    ppermute x17, starting transfers between devices, hop(): return lax.ppermute(value, ('tok', 'vocab'), pairs)  16.5 us
    ppermute x17, waiting for transfers between devices, hop(): return lax.ppermute(value, ('tok', 'vocab'), pairs)  11 us
    all_to_all x1, blocking collectives, body(): lax.all_to_all(packed, ('tok', 'vocab'), split_axis=0, concat_axis=0, til...  10.8 us
    pallas_call x2, Pallas kernels, body(): pl.pallas_call(functools.partial(load_kernel, part, plan), out_shape=stor...  7.68 us
    pallas_call x1, Pallas kernels, body(): pl.pallas_call(functools.partial(last_kernel, far_layout, len(far_arrays)...  6.37 us
    pallas_call x1, Pallas kernels, body(): pl.pallas_call(functools.partial(partial_kernel, layout, len(arrays), row...  4.61 us
  transfers between devices with their start and end apart: 17, of which 7 were waited for; matrix products, arithmetic and copies ran while one was open for 0% of the time, Pallas kernels for 21%

profile of v2, /device:TPU:0, one launch (start us, length us, event | category | flops | bytes accessed | tf_op | source)
XLA Modules:
  0.0 59.9 jit_solution(6357742545174734291)
XLA Ops:
  0.6 1.2 %own_columns.1 = bf16[24,9344]{1,0:T(8,128)(2,1)S(1)} custom-call(bf16[24,9216]{1,0:T(8,128)(2,1)} %hidden_ref.1, s32[1,24]{1,0:T(1,128)} %bitcast.4), custom_call_target="tpu_custom_call" | custom-call | tf_op jit(solution)/shard_map/own_columns/pallas_call | solution.py:59
  1.8 3.1 %collective-permute-start.1 = (bf16[24,2432]{1,0:T(8,128)(2,1)S(1)}, bf16[24,2432]{1,0:T(8,128)(2,1)S(1)}, u32[]{:S(2)}, u32[]{:S(2)}) collective-permute-start(bf16[24,2432]{1,0:T(8,128)(2,1)S(1)} %slice.52.refs_3_.refs_10_), channel_id=1, source_target_pairs={{0,8},{1,9},{2,10},{3,11},{4,12},{5,13},{6,14},{7,15},{8,0},{9,1},... | collective-permute-start | bytes 350216 | tf_op jit(solution)/shard_map/ppermute | solution.py:23
  4.9 2.6 %collective-permute-start.3 = (bf16[24,2432]{1,0:T(8,128)(2,1)S(1)}, bf16[24,2432]{1,0:T(8,128)(2,1)S(1)}, u32[]{:S(2)}, u32[]{:S(2)}) collective-permute-start(bf16[24,2432]{1,0:T(8,128)(2,1)S(1)} %slice.52.refs_3_.refs_10_), channel_id=1, source_target_pairs={{0,16},{1,17},{2,18},{3,19},{4,20},{5,21},{6,22},{7,23},{8,24},{9,... | collective-permute-start | bytes 350216 | tf_op jit(solution)/shard_map/ppermute | solution.py:23
  7.5 1.5 %collective-permute-start = (bf16[24,2432]{1,0:T(8,128)(2,1)S(1)}, bf16[24,2432]{1,0:T(8,128)(2,1)S(1)}, u32[]{:S(2)}, u32[]{:S(2)}) collective-permute-start(bf16[24,2432]{1,0:T(8,128)(2,1)S(1)} %slice.52.refs_3_.refs_10_), channel_id=1, source_target_pairs={{0,4},{1,5},{2,6},{3,7},{4,0},{5,1},{6,2},{7,3},{8,12},{9,13},{10,... | collective-permute-start | bytes 350216 | tf_op jit(solution)/shard_map/ppermute | solution.py:23
  9.1 0.3 collective-permute-done.1.refs_5_.refs_12_
  9.4 3.0 %collective-permute-done.refs_7_.refs_14_ = bf16[24,2432]{1,0:T(8,128)(2,1)S(1)} collective-permute-done((bf16[24,2432]{1,0:T(8,128)(2,1)S(1)}, bf16[24,2432]{1,0:T(8,128)(2,1)S(1)}, u32[]{:S(2)}, u32[]{:S(2)}) %collective-permute-start) | collective-permute-done | bytes 116768 | tf_op jit(solution)/shard_map/ppermute | solution.py:23
  12.3 1.6 %collective-permute-start.6 = (bf16[24,2432]{1,0:T(8,128)(2,1)S(1)}, bf16[24,2432]{1,0:T(8,128)(2,1)S(1)}, u32[]{:S(2)}, u32[]{:S(2)}) collective-permute-start(bf16[24,2432]{1,0:T(8,128)(2,1)S(1)} %collective-permute-done.1.refs_5_.refs_12_), channel_id=1, source_target_pairs={{0,4},{1,5},{2,6},{3,7},{4,0},{5,1},{6,2},{7,3},{8,12},{9,13},{10,... | collective-permute-start | bytes 350216 | tf_op jit(solution)/shard_map/ppermute | solution.py:23
  13.9 1.6 %collective-permute-start.2 = (bf16[48,2304]{1,0:T(8,128)(2,1)S(1)}, bf16[48,2304]{1,0:T(8,128)(2,1)S(1)}, u32[]{:S(2)}, u32[]{:S(2)}) collective-permute-start(bf16[48,2304]{1,0:T(8,128)(2,1)S(1)} %pad_maximum_fusion.3), channel_id=1, source_target_pairs={{0,2},{1,3},{2,0},{3,1},{4,6},{5,7},{6,4},{7,5},{8,10},{9,11},{10,... | collective-permute-start | bytes 663560 | tf_op jit(solution)/shard_map/ppermute | solution.py:23
  15.5 0.0 collective-permute-done.3.refs_4_.refs_11_
  15.5 0.6 %collective-permute-start.4 = (bf16[24,2304]{1,0:T(8,128)(2,1)S(1)}, bf16[24,2304]{1,0:T(8,128)(2,1)S(1)}, u32[]{:S(2)}, u32[]{:S(2)}) collective-permute-start(bf16[24,2304]{1,0:T(8,128)(2,1)S(1)} %slice.55), channel_id=1, source_target_pairs={{0,2},{1,3},{2,0},{3,1},{4,6},{5,7},{6,4},{7,5},{8,10},{9,11},{10,... | collective-permute-start | bytes 331784 | tf_op jit(solution)/shard_map/ppermute | solution.py:23
  16.1 0.4 collective-permute-start.5
  16.6 0.5 collective-permute-start.7
  17.1 1.1 %collective-permute-done.6.refs_9_.refs_16_ = bf16[24,2432]{1,0:T(8,128)(2,1)S(1)} collective-permute-done((bf16[24,2432]{1,0:T(8,128)(2,1)S(1)}, bf16[24,2432]{1,0:T(8,128)(2,1)S(1)}, u32[]{:S(2)}, u32[]{:S(2)}) %collective-permute-start.6) | collective-permute-done | bytes 116768 | tf_op jit(solution)/shard_map/ppermute | solution.py:23
  18.2 0.1 collective-permute-start.15
  18.3 2.7 %collective-permute-done.5.refs_6_.refs_13_ = bf16[24,2432]{1,0:T(8,128)(2,1)S(1)} collective-permute-done((bf16[24,2432]{1,0:T(8,128)(2,1)S(1)}, bf16[24,2432]{1,0:T(8,128)(2,1)S(1)}, u32[]{:S(2)}, u32[]{:S(2)}) %collective-permute-start.5) | collective-permute-done | bytes 116768 | tf_op jit(solution)/shard_map/ppermute | solution.py:23
  20.9 0.4 collective-permute-done.7.refs_8_.refs_15_
  21.4 0.6 collective-permute-start.9
  22.0 1.6 %collective-permute-start.8 = (bf16[72,2304]{1,0:T(8,128)(2,1)S(1)}, bf16[72,2304]{1,0:T(8,128)(2,1)S(1)}, u32[]{:S(2)}, u32[]{:S(2)}) collective-permute-start(bf16[72,2304]{1,0:T(8,128)(2,1)S(1)} %pad_maximum_fusion.1), channel_id=1, source_target_pairs={{0,2},{1,3},{2,0},{3,1},{4,6},{5,7},{6,4},{7,5},{8,10},{9,11},{10,... | collective-permute-start | bytes 995336 | tf_op jit(solution)/shard_map/ppermute | solution.py:23
  23.6 2.7 %collective-permute-done.9.refs_10_.refs_17_ = bf16[24,2432]{1,0:T(8,128)(2,1)S(1)} collective-permute-done((bf16[24,2432]{1,0:T(8,128)(2,1)S(1)}, bf16[24,2432]{1,0:T(8,128)(2,1)S(1)}, u32[]{:S(2)}, u32[]{:S(2)}) %collective-permute-start.9) | collective-permute-done | bytes 116768 | tf_op jit(solution)/shard_map/ppermute | solution.py:23
  26.3 0.1 collective-permute-start.16
  26.4 4.8 %load_heads.2.refs_0_ = bf16[2,6912,1024]{2,1,0:T(8,128)(2,1)S(1)} custom-call(bf16[9216,1024]{1,0:T(8,128)(2,1)} %refs_21_.1, bf16[9216,1024]{1,0:T(8,128)(2,1)} %refs_22_.1), custom_call_target="tpu_custom_call" | custom-call | flops 2415919104 | tf_op jit(solution)/shard_map/load_heads/pallas_call | solution.py:336
  31.2 0.0 collective-permute-done.4.refs_2_
  31.2 1.5 %collective-permute-start.10 = (bf16[24,2304]{1,0:T(8,128)(2,1)S(1)}, bf16[24,2304]{1,0:T(8,128)(2,1)S(1)}, u32[]{:S(2)}, u32[]{:S(2)}) collective-permute-start(bf16[24,2304]{1,0:T(8,128)(2,1)S(1)} %slice.59), channel_id=1, source_target_pairs={{0,2},{1,3},{2,0},{3,1},{4,6},{5,7},{6,4},{7,5},{8,10},{9,11},{10,... | collective-permute-start | bytes 331784 | tf_op jit(solution)/shard_map/ppermute | solution.py:23
  32.7 2.9 %load_heads.3.refs_0_ = bf16[2,6912,1024]{2,1,0:T(8,128)(2,1)S(1)} custom-call(bf16[9216,1024]{1,0:T(8,128)(2,1)} %refs_21_.1, bf16[9216,1024]{1,0:T(8,128)(2,1)} %refs_22_.1, bf16[2,6912,1024]{2,1,0:T(8,128)(2,1)S(1)} %load_heads.2.refs_0_), custom_call_target="tpu_custom_call", output_to_operand_aliasing={{}: (2, {})} | custom-call | flops 1207959552 | tf_op jit(solution)/shard_map/load_heads/pallas_call | solution.py:336
  35.6 0.0 collective-permute-done.2.refs_1_
  35.6 0.2 collective-permute-start.12
  35.8 0.8 %collective-permute-done.10.refs_4_ = bf16[24,2304]{1,0:T(8,128)(2,1)S(1)} collective-permute-done((bf16[24,2304]{1,0:T(8,128)(2,1)S(1)}, bf16[24,2304]{1,0:T(8,128)(2,1)S(1)}, u32[]{:S(2)}, u32[]{:S(2)}) %collective-permute-start.10) | collective-permute-done | bytes 110624 | tf_op jit(solution)/shard_map/ppermute | solution.py:23
  36.6 0.0 collective-permute-start.11
  36.6 0.0 collective-permute-done.8.refs_3_
  36.6 0.5 collective-permute-start.14
  37.2 0.0 collective-permute-done.15.refs_12_
  37.2 0.1 collective-permute-start.13
  37.2 0.0 collective-permute-done.16.refs_13_
  37.2 4.6 %first_part.1 = (f32[192,1024]{1,0:T(8,128)S(1)}, f32[192,1024]{1,0:T(8,128)S(1)}, bf16[2,6912,1024]{2,1,0:T(8,128)(2,1)S(1)}) custom-call(bf16[2,6912,1024]{2,1,0:T(8,128)(2,1)S(1)} %load_heads.3.refs_0_, bf16[9216,1024]{1,0:T(8,128)(2,1)} %refs_21_.1, bf16[9216,1024]{1,0:T(8,128)(2,1)} %refs_22_.1, ...), custom_call_target="tpu_custom_call", output_to_operand_aliasing={{2}: (0, {})} | custom-call | flops 3623878656 | tf_op jit(solution)/shard_map/first_part/pallas_call | solution.py:348
  41.8 0.0 collective-permute-done.12.refs_7_
  41.9 0.0 collective-permute-done.11.refs_6_
  41.9 0.0 collective-permute-done.14.refs_9_
  41.9 0.0 collective-permute-done.13.refs_8_
  41.9 6.4 %last_part.1 = f32[32,1,256]{2,1,0:T(1,128)S(1)} custom-call(bf16[24,2304]{1,0:T(8,128)(2,1)S(1)} %get-tuple-element.41.refs_0_, bf16[48,2304]{1,0:T(8,128)(2,1)S(1)} %collective-permute-done.2.refs_1_, bf16[24,2304]{1,0:T(8,128)(2,1)S(1)} %collective-permute-done.4.refs_2_, bf16[72,2304]{1,0:T(8,128)(2,1)S(1)} %collective-permute-done.8.refs_3_, ...), custom_call_target="tpu_custom_call" | custom-call | flops 3623878656 | tf_op jit(solution)/shard_map/last_part/pallas_call | solution.py:367
  48.3 10.8 %all_to_all.5.got_ref = f32[32,1,256]{2,1,0:T(1,128)S(1)} all-to-all(f32[32,1,256]{2,1,0:T(1,128)S(1)} %last_part.1), channel_id=1, replica_groups=mesh['tok'=8,'vocab'=4] {'tok','vocab'}, dimensions={0} | all-to-all | bytes 65536 | tf_op jit(solution)/shard_map/all_to_all | solution.py:392
  59.1 0.8 %finish.1 = (f32[1,24]{1,0:T(1,128)}, f32[1,24]{1,0:T(1,128)}, f32[1,24]{1,0:T(1,128)}) custom-call(f32[32,1,256]{2,1,0:T(1,128)S(1)} %all_to_all.5.got_ref), custom_call_target="tpu_custom_call" | custom-call | tf_op jit(solution)/shard_map/finish/pallas_call | solution.py:393
  (13 shorter events, 0.2 us)
Async XLA Ops:
  1.8 7.6 %collective-permute-start.1 = (bf16[24,2432]{1,0:T(8,128)(2,1)S(1)}, bf16[24,2432]{1,0:T(8,128)(2,1)S(1)}, u32[]{:S(2)}, u32[]{:S(2)}) collective-permute-start(bf16[24,2432]{1,0:T(8,128)(2,1)S(1)} %slice.52.refs_3_.refs_10_), channel_id=1, source_target_pairs={{0,8},{1,9},{2,10},{3,11},{4,12},{5,13},{6,14},{7,15},{8,0},{9,1},... | collective-permute-start | bytes 350216 | tf_op jit(solution)/shard_map/ppermute | solution.py:23
  4.9 10.6 %collective-permute-start.3 = (bf16[24,2432]{1,0:T(8,128)(2,1)S(1)}, bf16[24,2432]{1,0:T(8,128)(2,1)S(1)}, u32[]{:S(2)}, u32[]{:S(2)}) collective-permute-start(bf16[24,2432]{1,0:T(8,128)(2,1)S(1)} %slice.52.refs_3_.refs_10_), channel_id=1, source_target_pairs={{0,16},{1,17},{2,18},{3,19},{4,20},{5,21},{6,22},{7,23},{8,24},{9,... | collective-permute-start | bytes 350216 | tf_op jit(solution)/shard_map/ppermute | solution.py:23
  7.5 4.8 %collective-permute-start = (bf16[24,2432]{1,0:T(8,128)(2,1)S(1)}, bf16[24,2432]{1,0:T(8,128)(2,1)S(1)}, u32[]{:S(2)}, u32[]{:S(2)}) collective-permute-start(bf16[24,2432]{1,0:T(8,128)(2,1)S(1)} %slice.52.refs_3_.refs_10_), channel_id=1, source_target_pairs={{0,4},{1,5},{2,6},{3,7},{4,0},{5,1},{6,2},{7,3},{8,12},{9,13},{10,... | collective-permute-start | bytes 350216 | tf_op jit(solution)/shard_map/ppermute | solution.py:23
  12.3 5.8 %collective-permute-start.6 = (bf16[24,2432]{1,0:T(8,128)(2,1)S(1)}, bf16[24,2432]{1,0:T(8,128)(2,1)S(1)}, u32[]{:S(2)}, u32[]{:S(2)}) collective-permute-start(bf16[24,2432]{1,0:T(8,128)(2,1)S(1)} %collective-permute-done.1.refs_5_.refs_12_), channel_id=1, source_target_pairs={{0,4},{1,5},{2,6},{3,7},{4,0},{5,1},{6,2},{7,3},{8,12},{9,13},{10,... | collective-permute-start | bytes 350216 | tf_op jit(solution)/shard_map/ppermute | solution.py:23
  13.9 21.6 %collective-permute-start.2 = (bf16[48,2304]{1,0:T(8,128)(2,1)S(1)}, bf16[48,2304]{1,0:T(8,128)(2,1)S(1)}, u32[]{:S(2)}, u32[]{:S(2)}) collective-permute-start(bf16[48,2304]{1,0:T(8,128)(2,1)S(1)} %pad_maximum_fusion.3), channel_id=1, source_target_pairs={{0,2},{1,3},{2,0},{3,1},{4,6},{5,7},{6,4},{7,5},{8,10},{9,11},{10,... | collective-permute-start | bytes 663560 | tf_op jit(solution)/shard_map/ppermute | solution.py:23
  15.5 15.7 %collective-permute-start.4 = (bf16[24,2304]{1,0:T(8,128)(2,1)S(1)}, bf16[24,2304]{1,0:T(8,128)(2,1)S(1)}, u32[]{:S(2)}, u32[]{:S(2)}) collective-permute-start(bf16[24,2304]{1,0:T(8,128)(2,1)S(1)} %slice.55), channel_id=1, source_target_pairs={{0,2},{1,3},{2,0},{3,1},{4,6},{5,7},{6,4},{7,5},{8,10},{9,11},{10,... | collective-permute-start | bytes 331784 | tf_op jit(solution)/shard_map/ppermute | solution.py:23
  16.1 4.8 %collective-permute-start.5 = (bf16[24,2432]{1,0:T(8,128)(2,1)S(1)}, bf16[24,2432]{1,0:T(8,128)(2,1)S(1)}, u32[]{:S(2)}, u32[]{:S(2)}) collective-permute-start(bf16[24,2432]{1,0:T(8,128)(2,1)S(1)} %collective-permute-done.3.refs_4_.refs_11_), channel_id=1, source_target_pairs={{0,8},{1,9},{2,10},{3,11},{4,12},{5,13},{6,14},{7,15},{8,0},{9,1},... | collective-permute-start | bytes 350216 | tf_op jit(solution)/shard_map/ppermute | solution.py:23
  16.6 4.8 %collective-permute-start.7 = (bf16[24,2432]{1,0:T(8,128)(2,1)S(1)}, bf16[24,2432]{1,0:T(8,128)(2,1)S(1)}, u32[]{:S(2)}, u32[]{:S(2)}) collective-permute-start(bf16[24,2432]{1,0:T(8,128)(2,1)S(1)} %collective-permute-done.3.refs_4_.refs_11_), channel_id=1, source_target_pairs={{0,4},{1,5},{2,6},{3,7},{4,0},{5,1},{6,2},{7,3},{8,12},{9,13},{10,... | collective-permute-start | bytes 350216 | tf_op jit(solution)/shard_map/ppermute | solution.py:23
  18.2 19.0 %collective-permute-start.15 = (bf16[96,2304]{1,0:T(8,128)(2,1)S(1)}, bf16[96,2304]{1,0:T(8,128)(2,1)S(1)}, u32[]{:S(2)}, u32[]{:S(2)}) collective-permute-start(bf16[96,2304]{1,0:T(8,128)(2,1)S(1)} %pad_maximum_fusion), channel_id=1, source_target_pairs={{0,1},{1,0},{2,3},{3,2},{4,5},{5,4},{6,7},{7,6},{8,9},{9,8},{10,11... | collective-permute-start | bytes 1327112 | tf_op jit(solution)/shard_map/ppermute | solution.py:23
  21.4 4.9 %collective-permute-start.9 = (bf16[24,2432]{1,0:T(8,128)(2,1)S(1)}, bf16[24,2432]{1,0:T(8,128)(2,1)S(1)}, u32[]{:S(2)}, u32[]{:S(2)}) collective-permute-start(bf16[24,2432]{1,0:T(8,128)(2,1)S(1)} %collective-permute-done.5.refs_6_.refs_13_), channel_id=1, source_target_pairs={{0,4},{1,5},{2,6},{3,7},{4,0},{5,1},{6,2},{7,3},{8,12},{9,13},{10,... | collective-permute-start | bytes 350216 | tf_op jit(solution)/shard_map/ppermute | solution.py:23
  22.0 14.7 %collective-permute-start.8 = (bf16[72,2304]{1,0:T(8,128)(2,1)S(1)}, bf16[72,2304]{1,0:T(8,128)(2,1)S(1)}, u32[]{:S(2)}, u32[]{:S(2)}) collective-permute-start(bf16[72,2304]{1,0:T(8,128)(2,1)S(1)} %pad_maximum_fusion.1), channel_id=1, source_target_pairs={{0,2},{1,3},{2,0},{3,1},{4,6},{5,7},{6,4},{7,5},{8,10},{9,11},{10,... | collective-permute-start | bytes 995336 | tf_op jit(solution)/shard_map/ppermute | solution.py:23
  26.3 10.9 %collective-permute-start.16 = (bf16[72,2304]{1,0:T(8,128)(2,1)S(1)}, bf16[72,2304]{1,0:T(8,128)(2,1)S(1)}, u32[]{:S(2)}, u32[]{:S(2)}) collective-permute-start(bf16[72,2304]{1,0:T(8,128)(2,1)S(1)} %pad_maximum_fusion.2), channel_id=1, source_target_pairs={{0,1},{1,0},{2,3},{3,2},{4,5},{5,4},{6,7},{7,6},{8,9},{9,8},{10,11... | collective-permute-start | bytes 995336 | tf_op jit(solution)/shard_map/ppermute | solution.py:23
  31.2 5.4 %collective-permute-start.10 = (bf16[24,2304]{1,0:T(8,128)(2,1)S(1)}, bf16[24,2304]{1,0:T(8,128)(2,1)S(1)}, u32[]{:S(2)}, u32[]{:S(2)}) collective-permute-start(bf16[24,2304]{1,0:T(8,128)(2,1)S(1)} %slice.59), channel_id=1, source_target_pairs={{0,2},{1,3},{2,0},{3,1},{4,6},{5,7},{6,4},{7,5},{8,10},{9,11},{10,... | collective-permute-start | bytes 331784 | tf_op jit(solution)/shard_map/ppermute | solution.py:23
  35.6 6.3 %collective-permute-start.12 = (bf16[24,2304]{1,0:T(8,128)(2,1)S(1)}, bf16[24,2304]{1,0:T(8,128)(2,1)S(1)}, u32[]{:S(2)}, u32[]{:S(2)}) collective-permute-start(bf16[24,2304]{1,0:T(8,128)(2,1)S(1)} %collective-permute-done.4.refs_2_), channel_id=1, source_target_pairs={{0,1},{1,0},{2,3},{3,2},{4,5},{5,4},{6,7},{7,6},{8,9},{9,8},{10,11... | collective-permute-start | bytes 331784 | tf_op jit(solution)/shard_map/ppermute | solution.py:23
  36.6 5.2 %collective-permute-start.11 = (bf16[48,2304]{1,0:T(8,128)(2,1)S(1)}, bf16[48,2304]{1,0:T(8,128)(2,1)S(1)}, u32[]{:S(2)}, u32[]{:S(2)}) collective-permute-start(bf16[48,2304]{1,0:T(8,128)(2,1)S(1)} %collective-permute-done.2.refs_1_), channel_id=1, source_target_pairs={{0,1},{1,0},{2,3},{3,2},{4,5},{5,4},{6,7},{7,6},{8,9},{9,8},{10,11... | collective-permute-start | bytes 663560 | tf_op jit(solution)/shard_map/ppermute | solution.py:23
  36.6 5.2 %collective-permute-start.14 = (bf16[24,2304]{1,0:T(8,128)(2,1)S(1)}, bf16[24,2304]{1,0:T(8,128)(2,1)S(1)}, u32[]{:S(2)}, u32[]{:S(2)}) collective-permute-start(bf16[24,2304]{1,0:T(8,128)(2,1)S(1)} %collective-permute-done.10.refs_4_), channel_id=1, source_target_pairs={{0,1},{1,0},{2,3},{3,2},{4,5},{5,4},{6,7},{7,6},{8,9},{9,8},{10,11... | collective-permute-start | bytes 331784 | tf_op jit(solution)/shard_map/ppermute | solution.py:23
  37.2 4.7 %collective-permute-start.13 = (bf16[72,2304]{1,0:T(8,128)(2,1)S(1)}, bf16[72,2304]{1,0:T(8,128)(2,1)S(1)}, u32[]{:S(2)}, u32[]{:S(2)}) collective-permute-start(bf16[72,2304]{1,0:T(8,128)(2,1)S(1)} %collective-permute-done.8.refs_3_), channel_id=1, source_target_pairs={{0,1},{1,0},{2,3},{3,2},{4,5},{5,4},{6,7},{7,6},{8,9},{9,8},{10,11... | collective-permute-start | bytes 995336 | tf_op jit(solution)/shard_map/ppermute | solution.py:23
